TPU v7x, 128 devices: a whole 4x4x4 slice. The times are simulated.
128 devices in a mesh: dp: 8 (over z, core), mp: 16 (over x, y).
Axes of the slice: x: 4, y: 4, z: 4, core: 2. Of those that a mesh axis runs over, the one named last changes fastest.
Arguments:
- features: bfloat16 [8192, 2048], P('dp'), may hold values from -21 to 21
- rewards: float32 [32, 256], P('dp'), may hold values from -6 to 6
- old_values: float32 [32, 256], P('dp'), may hold values from -6 to 6
- dones: int32 [32, 256], P('dp'), may hold values 0 or 1
- lengths: int32 [32], P('dp'), may hold values from 128 to 256
- proj_weights: bfloat16 [2048, 2, 8192], P(None, None, 'mp'), may hold values from -0.125 to 0.125
- down_weight: bfloat16 [8192, 2048], P('mp'), may hold values from -0.0625 to 0.0625
- value_head: float32 [2048], replicated, may hold values from -0.0078125 to 0.0078125
- master: float32 [2048, 2, 8192], P('dp', None, 'mp'), may hold values from -0.125 to 0.125
- moment: float32 [2048, 2, 8192], P('dp', None, 'mp'), may hold values from -1.035801e-05 to 1.035801e-05
- second: float32 [2048, 2, 8192], P('dp', None, 'mp'), may hold values from 2.9802322e-13 to 2.9802322e-12
Outputs:
- master_new: float32 [2048, 2, 8192], P('dp', None, 'mp')
- moment_new: float32 [2048, 2, 8192], P('dp', None, 'mp')
- second_new: float32 [2048, 2, 8192], P('dp', None, 'mp')
- working: bfloat16 [2048, 2, 8192], P(None, None, 'mp')
- total_loss: float32 [], replicated
All inputs are finite; a program needn't handle non-finite values. No bound on the sum of `dones` on one device may be relied on, other than what follows from the above.
Results may differ from a plain program's by a relative error of at most 0.0011.
Values may be sent and summed in bfloat16 or wider, within the bound.
A program may use at most 128 MiB of HBM per device.

v0:
```python
import functools
import math

import jax
import jax.numpy as jnp
from jax import lax
from jax.sharding import Mesh
from jax.sharding import PartitionSpec as P

DP = ("dp_0", "dp_1")
MP = ("mp_0", "mp_1")
DP_MP = ("dp_0", "dp_1", "mp_0", "mp_1")


GAMMA = 0.99
LAMBDA = 0.95
MAX_NORM = 0.05


def own_block(parts, axes, sequence):
    shape = [lax.axis_size(a) for a in axes]
    parts = parts.reshape(*shape, *parts.shape[1:])
    parts = parts.transpose(*sequence, *range(len(axes), parts.ndim))
    parts = parts.reshape(-1, *parts.shape[len(axes) :])
    for k in sequence:
        parts = lax.psum_scatter(parts, axes[k], scatter_dimension=0, tiled=True)
    return parts[0]


def in_blocks(value, dim, count):
    before, after = (value.shape[:dim], value.shape[dim + 1 :])
    return jnp.moveaxis(value.reshape(*before, count, -1, *after), dim, 0)


def summed_rows(value, axes, sequence, dim):
    count = lax.axis_size(axes)
    return own_block(in_blocks(value, dim, count), axes, sequence)


def one_axis_at_a_time(value, axes):
    return functools.reduce(lax.psum, axes, value)


def gae_targets(rewards, old_values, dones, lengths):
    seq_len = rewards.shape[1]
    keeps = 1.0 - dones.astype(jnp.float32)
    following = jnp.concatenate([old_values[:, 1:], jnp.zeros_like(old_values[:, :1])], axis=1)
    deltas = rewards + GAMMA * following * keeps - old_values
    counted = jnp.cumsum(dones, axis=1) - dones
    places = jnp.arange(seq_len, dtype=jnp.int32)
    spans = places[None, :] - places[:, None]
    linked = (counted[:, :, None] == counted[:, None, :]) & (spans[None] >= 0)
    powers = jnp.exp(jnp.maximum(spans, 0).astype(jnp.float32) * math.log(GAMMA * LAMBDA))
    kernel = jnp.where(linked, powers[None], jnp.zeros((), jnp.float32))
    advantage = jnp.einsum("ats,as->at", kernel, deltas, precision=lax.Precision.HIGHEST)
    targets = (advantage + old_values).reshape(-1)
    mask = (places[None, :] < lengths[:, None]).astype(jnp.float32).reshape(-1)
    return (targets, mask)


def value_loss(features, mixed, targets, mask, value_head, total_tokens):
    stream = features.astype(jnp.float32) + mixed
    norm_factor = lax.rsqrt(jnp.mean(stream * stream, axis=-1) + 1e-05)
    normed = stream * norm_factor[:, None]
    estimate = jnp.dot(normed, value_head, precision=lax.Precision.HIGHEST)
    errors = estimate - targets
    loss_part = jnp.sum(mask * errors * errors) / total_tokens
    coeff = 2.0 * mask * errors / total_tokens
    head_grad = coeff[:, None] * value_head[None, :]
    out_grad = (
        norm_factor[:, None]
        * (head_grad - normed * jnp.mean(head_grad * normed, axis=-1, keepdims=True))
    ).astype(jnp.bfloat16)
    return (loss_part, out_grad)


def contract_rows(left, right):
    return lax.dot_general(
        left, right, (((0,), (0,)), ((), ())), preferred_element_type=jnp.float32
    )


def per_device(
    features,
    rewards,
    old_values,
    dones,
    lengths,
    proj_weights,
    down_weight,
    value_head,
    master,
    moment,
    second,
):
    token_count = features.shape[0]
    model_width = features.shape[1]
    ff_local = down_weight.shape[0]
    data_ways = lax.axis_size(DP)
    model_ways = lax.axis_size(MP)
    total_tokens = token_count * data_ways
    targets, mask = gae_targets(rewards, old_values, dones, lengths)
    both = jnp.dot(
        features,
        proj_weights.reshape(model_width, 2 * ff_local),
        preferred_element_type=jnp.float32,
    )
    both = both.reshape(token_count, 2, ff_local)
    gate_values = both[:, 0, :]
    up_values = both[:, 1, :]
    hidden = (jax.nn.silu(gate_values) * up_values).astype(jnp.bfloat16)
    mixed = lax.psum(
        jnp.dot(hidden, down_weight, preferred_element_type=jnp.float32).astype(jnp.bfloat16), MP
    ).astype(jnp.float32)
    loss_part, out_grad = value_loss(features, mixed, targets, mask, value_head, total_tokens)
    loss_part = loss_part / model_ways
    hidden_grad = jnp.dot(out_grad, down_weight.T, preferred_element_type=jnp.float32)
    gate_sigmoid = jax.nn.sigmoid(gate_values)
    gate_grad = (
        hidden_grad * up_values * gate_sigmoid * (1.0 + gate_values * (1.0 - gate_sigmoid))
    ).astype(jnp.bfloat16)
    up_grad = (hidden_grad * gate_values * gate_sigmoid).astype(jnp.bfloat16)
    both_grad = jnp.stack([gate_grad, up_grad], axis=1).reshape(token_count, 2 * ff_local)
    row_share = model_width // data_ways
    grads = summed_rows(
        contract_rows(features, both_grad).reshape(row_share * lax.axis_size(DP), 2, ff_local),
        DP,
        (1, 0),
        0,
    )
    squares = jnp.sum(grads * grads)
    squared_total, total_loss = (
        one_axis_at_a_time(squares, DP_MP),
        one_axis_at_a_time(loss_part, DP_MP),
    )
    clip = jnp.minimum(1.0, MAX_NORM / (jnp.sqrt(squared_total) + 1e-06))
    clipped = clip * grads
    moment_new = 0.9 * moment + 0.1 * clipped
    second_new = 0.999 * second + 0.001 * clipped * clipped
    first_hat = moment_new / (1.0 - 0.9**10)
    second_hat = second_new / (1.0 - 0.999**10)
    master_new = master - 0.001 * (first_hat / (jnp.sqrt(second_hat) + 1e-08) + 0.1 * master)
    working = lax.all_gather(master_new.astype(jnp.bfloat16), DP, axis=0, tiled=True)
    return (master_new, moment_new, second_new, working, total_loss)


def solution(mesh):
    finer = Mesh(mesh.devices.reshape(4, 2, 4, 4), ("dp_0", "dp_1", "mp_0", "mp_1"))
    return jax.shard_map(
        per_device,
        mesh=finer,
        in_specs=(
            P(DP, None),
            P(DP, None),
            P(DP, None),
            P(DP, None),
            P(DP),
            P(None, None, MP),
            P(MP, None),
            P(),
            P(DP, None, MP),
            P(DP, None, MP),
            P(DP, None, MP),
        ),
        out_specs=(P(DP, None, MP), P(DP, None, MP), P(DP, None, MP), P(None, None, MP), P()),
        check_vma=False,
    )
```

profile of v0, /device:TPU:1, one launch (start us, length us, event | category | flops | bytes accessed | tf_op | source)
XLA Modules:
  0.0 348.5 jit_solution(17223176488133655442)
XLA Ops:
  7.2 0.0 all-reduce.7.cloned.1.call-start
  7.2 5.5 %copy.34 = bf16[256,8,2,512]{3,1,2,0:T(8,128)(2,1)} copy(bf16[256,8,2,512]{3,2,1,0:T(2,128)(2,1)} %bitcast.73) | data formatting | bytes 8388608
  12.8 6.5 %copy.21 = bf16[1024,2048]{1,0:T(8,128)(2,1)} copy(bf16[1024,2048]{0,1:T(8,128)(2,1)} %bitcast.72) | data formatting | bytes 8388608 | tf_op jit(solution)/shard_map/dot_general | solution.py:103
  19.3 7.6 %fusion.6 = f32[1024,2,512]{0,2,1:T(8,128)S(1)} fusion(bf16[2,512,2048]{2,1,0:T(8,128)(2,1)} %bitcast.74, bf16[1024,2048]{1,0:T(8,128)(2,1)} %param.11), kind=kOutput, calls=%fused_computation.10 | convolution fusion | flops 4294967296 | bytes 12582912 | tf_op jit(solution)/shard_map/dot_general | solution.py:103
  26.9 2.0 copy-done.9
  28.9 4.4 %convolution_convert_fusion = bf16[1024,2048]{1,0:T(8,128)(2,1)} fusion(bf16[512,2048]{1,0:T(8,128)(2,1)S(1)} %copy-done, f32[1024,2,512]{0,2,1:T(8,128)S(1)} %fusion.6), kind=kOutput, calls=%fused_computation.14 | convolution fusion | flops 2152726528 | bytes 10485760 | tf_op jit(solution)/shard_map/dot_general | solution.py:113
  33.3 0.0 all-reduce.7.cloned.1.call-update
  33.4 0.2 reduce-scatter.3.cloned.1.call-start
  33.6 0.4 copy-done.8
  34.0 0.1 iota_compare_fusion
  34.1 0.1 slice.19
  34.2 1.2 reduce-window.6
  35.4 0.1 slice.22
  35.4 0.1 copy.22
  35.6 0.1 copy.23
  35.7 0.1 multiply_exponential_fusion
  35.8 0.1 add_bitcast_fusion
  35.9 1.2 fusion.13
  37.1 102.5 %all-reduce.7.cloned.1.call-done = bf16[1024,2048]{1,0:T(8,128)(2,1)} async-done(((bf16[1024,2048]{1,0:T(8,128)(2,1)}), bf16[1024,2048]{1,0:T(8,128)(2,1)}) %all-reduce.7.cloned.1.call-update) | async-done | bytes 4194320 | tf_op jit(solution)/shard_map/psum | solution.py:112
  139.7 5.0 %multiply_reduce_fusion = f32[1024]{0:T(1024)S(1)} fusion(bf16[1024,2048]{1,0:T(8,128)(2,1)} %all-reduce.7.cloned.1.call-done, bf16[1024,2048]{1,0:T(8,128)(2,1)} %param.11), kind=kLoop, calls=%fused_computation.5 | loop fusion | flops 10484736 | bytes 8392704 | tf_op jit(solution)/shard_map/reduce_sum | solution.py:63
  144.7 0.9 copy-done.3
  145.6 8.1 %fusion.4 = f32[1,1024]{1,0:T(1,128)S(1)} fusion(f32[2048,1]{0,1:T(1,128)S(1)} %bitcast.76, bf16[1024,2048]{1,0:T(8,128)(2,1)S(1)} %copy-done.3, bf16[1024,2048]{1,0:T(8,128)(2,1)S(1)} %copy-done.2, f32[1024]{0:T(1024)S(1)} %add_rsqrt_fusion), kind=kOutput, calls=%fused_computation.8 | convolution fusion | flops 33554432 | bytes 8404992 | tf_op jit(solution)/shard_map/dot_general | solution.py:65
  153.7 0.6 fusion.26
  154.4 2.6 fusion
  156.9 5.4 %fusion.19 = (bf16[1024,1,512]{0,2,1:T(8,128)(2,1)S(1)}, bf16[1024,1,512]{0,2,1:T(8,128)(2,1)S(1)}) fusion(f32[1024,2,512]{0,2,1:T(8,128)S(1)} %copy-done.10, bf16[512,2048]{1,0:T(8,128)(2,1)S(1)} %copy-done, bf16[1024,2048]{1,0:T(8,128)(2,1)S(1)} %copy-done.3, bf16[1024,2048]{1,0:T(8,128)(2,1)S(1)} %copy-done.2, f32[1024]{0:T(1024)S(1)} %broadcast_multiply_fusion, ...), kind=kOutput, calls=%fused_computation.36 | convolution fusion | flops 2173173760 | bytes 16797696 | tf_op jit(solution)/shard_map/dot_general | solution.py:117
  162.4 0.2 pad_maximum_fusion
  162.6 6.7 %convolution_bitcast_fusion = f32[2048,1024]{0,1:T(8,128)} fusion(bf16[1024,1024]{0,1:T(8,128)(2,1)S(1)} %bitcast.75, bf16[1024,2048]{1,0:T(8,128)(2,1)S(1)} %copy-done.2), kind=kOutput, calls=%fused_computation.9 | convolution fusion | flops 4294967296 | bytes 14680064 | tf_op jit(solution)/shard_map/dot_general | solution.py:78
  169.3 11.7 %reshape_reshape_reshape.3 = f32[4,2,256,2,512]{2,1,0,4,3:T(2,128)} reshape(f32[2048,1024]{0,1:T(8,128)} %convolution_bitcast_fusion) | data formatting | bytes 16777216 | tf_op jit(solution)/shard_map/reshape;reshape;reshape | solution.py:22
  181.0 13.1 %copy.24 = f32[2,4,256,2,512]{4,2,3,1,0:T(8,128)} copy(f32[2,4,256,2,512]{2,0,1,4,3:T(2,128)} %bitcast.71) | data formatting | bytes 16777216 | tf_op jit(solution)/shard_map/transpose | solution.py:23
  194.1 0.0 reduce-scatter.3.cloned.1.call-update
  194.1 0.0 reduce-scatter.5.cloned.1.call-start
  194.2 19.7 %reduce-scatter.3.cloned.1.call-done = f32[4,256,2,512]{3,1,2,0:T(8,128)} async-done(((f32[8,256,2,512]{3,1,2,0:T(8,128)}), f32[4,256,2,512]{3,1,2,0:T(8,128)}) %reduce-scatter.3.cloned.1.call-update) | async-done | bytes 4194320 | tf_op jit(solution)/shard_map/reduce_scatter | solution.py:26
  213.9 0.0 reduce-scatter.5.cloned.1.call-update
  213.9 0.0 all-gather.2.cloned.1.call-start
  214.6 49.8 %reduce-scatter.5.cloned.1.call-done = f32[1,256,2,512]{3,1,2,0:T(8,128)} async-done(((f32[4,256,2,512]{3,1,2,0:T(8,128)}), f32[1,256,2,512]{3,1,2,0:T(8,128)}) %reduce-scatter.5.cloned.1.call-update) | async-done | bytes 1048592 | tf_op jit(solution)/shard_map/reduce_scatter | solution.py:26
  264.4 2.1 multiply_reduce_fusion.1
  266.5 7.1 %all-reduce.3 = (f32[]{:T(128)}, f32[]{:T(128)}) all-reduce(f32[]{:T(128)} %multiply_reduce_fusion.1, f32[]{:T(128)S(6)} %div.55), channel_id=1, replica_groups=mesh['dp_0'=4,'dp_1'=2,'mp_0'=4,'mp_1'=4] {'dp_0'}, use_global_device_ids=true, to_apply=%region_8.9 | all-reduce | flops 2 | bytes 16 | tf_op jit(solution)/shard_map/psum | solution.py:41
  273.6 5.5 %all-reduce.4 = (f32[]{:T(128)}, f32[]{:T(128)}) all-reduce(f32[]{:T(128)} %get-tuple-element.14, f32[]{:T(128)} %get-tuple-element.15), channel_id=1, replica_groups=mesh['dp_0'=4,'dp_1'=2,'mp_0'=4,'mp_1'=4] {'dp_1'}, use_global_device_ids=true, to_apply=%region_9.10 | all-reduce | flops 2 | bytes 16 | tf_op jit(solution)/shard_map/psum | solution.py:41
  279.1 9.0 %all-reduce.2 = (f32[]{:T(128)}, f32[]{:T(128)}) all-reduce(f32[]{:T(128)} %get-tuple-element.16, f32[]{:T(128)} %get-tuple-element.17), channel_id=1, replica_groups=mesh['dp_0'=4,'dp_1'=2,'mp_0'=4,'mp_1'=4] {'mp_0'}, use_global_device_ids=true, to_apply=%region_10.11 | all-reduce | flops 2 | bytes 16 | tf_op jit(solution)/shard_map/psum | solution.py:41
  288.1 9.1 %all-reduce.1 = (f32[]{:T(128)}, f32[]{:T(128)}) all-reduce(f32[]{:T(128)} %get-tuple-element.12, f32[]{:T(128)} %get-tuple-element.13), channel_id=1, replica_groups=mesh['dp_0'=4,'dp_1'=2,'mp_0'=4,'mp_1'=4] {'mp_1'}, use_global_device_ids=true, to_apply=%region_11.12 | all-reduce | flops 2 | bytes 16 | tf_op jit(solution)/shard_map/psum | solution.py:41
  297.9 3.2 fusion.31
  301.1 1.3 copy.28
  302.4 0.0 all-gather.2.cloned.1.call-update
  302.5 1.8 copy.29
  304.2 1.8 copy.30
  306.0 1.8 copy.31
  307.8 26.3 %all-gather.2.cloned.1.call-done = bf16[2048,2,512]{2,1,0:T(2,128)(2,1)} async-done(((bf16[256,2,512]{2,1,0:T(2,128)(2,1)}), bf16[2048,2,512]{2,1,0:T(2,128)(2,1)}) %all-gather.2.cloned.1.call-update) | async-done | bytes 4194320 | tf_op jit(solution)/shard_map/all_gather | solution.py:143
  334.1 7.8 %copy.53 = bf16[2048,2,512]{2,1,0:T(2,128)(2,1)} copy(bf16[2048,2,512]{2,1,0:T(2,128)(2,1)} %all-gather.2.cloned.1.call-done) | data formatting | bytes 8388608
  (30 shorter events, 0.2 us)
Async XLA Ops:
  7.2 21.7 %copy-start = (bf16[512,2048]{1,0:T(8,128)(2,1)S(1)}, bf16[512,2048]{1,0:T(8,128)(2,1)}, u32[]{:S(2)}) copy-start(bf16[512,2048]{1,0:T(8,128)(2,1)} %param.17) | copy-start | bytes 6291460
  7.2 132.5 %all-reduce.7.cloned.1.call-start = ((), (), s32[]{:S(2)}) async-start(), calls=%async_computation.2 | async-start | bytes 8388608 | tf_op jit(solution)/shard_map/psum | solution.py:112
  26.9 2.0 copy-start.9
  33.3 0.7 copy-start.8
  33.3 0.7 copy-start.5
  33.3 0.8 copy-start.4
  33.3 2.5 copy-start.7
  33.4 180.5 %reduce-scatter.3.cloned.1.call-start = ((), (), s32[]{:S(2)}) async-start(), calls=%async_computation.3 | async-start | bytes 12582912 | tf_op jit(solution)/shard_map/reduce_scatter | solution.py:26
  37.1 107.6 %copy-start.6 = (f32[2048]{0:T(1024)S(1)}, f32[2048]{0:T(1024)}, u32[]{:S(2)}) copy-start(f32[2048]{0:T(1024)} %param.18) | copy-start | bytes 24580
  139.7 5.1 %copy-start.2 = (bf16[1024,2048]{1,0:T(8,128)(2,1)S(1)}, bf16[1024,2048]{1,0:T(8,128)(2,1)}, u32[]{:S(2)}) copy-start(bf16[1024,2048]{1,0:T(8,128)(2,1)} %param.11) | copy-start | bytes 12582916
  139.7 5.9 %copy-start.3 = (bf16[1024,2048]{1,0:T(8,128)(2,1)S(1)}, bf16[1024,2048]{1,0:T(8,128)(2,1)}, u32[]{:S(2)}) copy-start(bf16[1024,2048]{1,0:T(8,128)(2,1)} %all-reduce.7.cloned.1.call-done) | copy-start | bytes 12582916
  154.3 2.6 copy-start.10
  194.1 70.3 %reduce-scatter.5.cloned.1.call-start = ((), (), s32[]{:S(2)}) async-start(), calls=%async_computation.4 | async-start | bytes 5242880 | tf_op jit(solution)/shard_map/reduce_scatter | solution.py:26
  213.9 120.2 %all-gather.2.cloned.1.call-start = ((), (), s32[]{:S(2)}) async-start(), calls=%async_computation.5 | async-start | bytes 4718592 | tf_op jit(solution)/shard_map/all_gather | solution.py:143
  334.1 7.9 %copy-start.1 = (bf16[512,2048]{1,0:T(8,128)(2,1)S(1)}, bf16[512,2048]{1,0:T(8,128)(2,1)}, u32[]{:S(2)}) copy-start(bf16[512,2048]{1,0:T(8,128)(2,1)} %param.17) | copy-start | bytes 6291460
Sparse Core Ops, SparseCore 0:
  33.5 106.1 all-reduce.6
  194.2 19.5 reduce-scatter.2
  216.3 48.0 reduce-scatter.4
  302.6 31.4 all-gather.1
where the time goes:
time: 350 us; the launch traced here: 348 us
  waiting for transfers between devices  198 us (57%)
  local copies, waits for them, and re-layouts  55.1 us (16%)
  matrix products  33.5 us (10%)
  blocking collectives  30.7 us (9%)
  other arithmetic  15.3 us (4%)
  between operations  15.3 us (4%)
    psum x1, waiting for transfers between devices, per_device(): lax.psum(jnp.dot(hidden, down_weight, preferred_element_type=jnp.float32)...  103 us
    reduce_scatter x2, waiting for transfers between devices, own_block(): parts = lax.psum_scatter(parts, axes[k], scatter_dimension=0, tiled=True)  69.5 us
    psum x4, blocking collectives, one_axis_at_a_time(): return functools.reduce(lax.psum, axes, value)  30.7 us
    all_gather x1, waiting for transfers between devices, per_device(): lax.all_gather(master_new.astype(jnp.bfloat16), DP, axis=0, tiled=True)  26.3 us
    unnamed x28, local copies, waits for them, and re-layouts  22 us
    transpose x1, local copies, waits for them, and re-layouts, own_block(): parts = parts.transpose(*sequence, *range(len(axes), parts.ndim))  13.1 us
    another operation x1, local copies, waits for them, and re-layouts, own_block(): parts = parts.reshape(*shape, *parts.shape[1:])  11.7 us
    dot_general x1, matrix products, value_loss(): estimate = jnp.dot(normed, value_head, precision=lax.Precision.HIGHEST)  8.13 us
  transfers between devices with their start and end apart: 4, of which 4 were waited for; matrix products, arithmetic and copies ran while one was open for 2% of the time, Pallas kernels for 0%

commit v1 on v0

v1 whole, which is shorter than its diff:
```python
import math

import jax
import jax.numpy as jnp
from jax import lax
from jax.experimental import pallas as pl
from jax.experimental.pallas import tpu as pltpu
from jax.sharding import Mesh
from jax.sharding import PartitionSpec as P

Z, CORE, X, Y = "dp_0", "dp_1", "mp_0", "mp_1"
DP = (Z, CORE)
MP = (X, Y)
GAMMA = 0.99
LAMBDA = 0.95
MAX_NORM = 0.05
D = 2048
TOK = 1024
FFL = 512
ROWS = 256
BF = jnp.bfloat16
LEVELS = 32000.0
F32 = jnp.float32
VMEM_LIMIT = 62 * 1024 * 1024


def mul_of(v, n):
    return pl.multiple_of(v, n)


def ring(v, d):
    return lax.rem(v + (d + 4), 4)


def remote(src, dst, send, recv, device):
    return pltpu.make_async_remote_copy(
        src_ref=src, dst_ref=dst, send_sem=send, recv_sem=recv,
        device_id=device, device_id_type=pl.DeviceIdType.MESH,
    )


def greet(devices):
    barrier = pltpu.get_barrier_semaphore()
    for device in devices:
        pl.semaphore_signal(barrier, inc=1, device_id=device, device_id_type=pl.DeviceIdType.MESH)
    pl.semaphore_wait(barrier, len(devices))


def own_targets(x, y, rew, old, dones, lengths):
    dn = jnp.broadcast_to(dones[pl.ds(y, 1), :].astype(F32), (8, 256))
    ov = jnp.broadcast_to(old[pl.ds(y, 1), :], (8, 256))
    rw = jnp.broadcast_to(rew[pl.ds(y, 1), :], (8, 256))
    lane = lax.broadcasted_iota(jnp.int32, (8, 256), 1)
    following = jnp.where(lane == 255, 0.0, pltpu.roll(ov, 255, axis=1))
    deltas = (rw + GAMMA * following * (1.0 - dn) - ov)[0:1]
    before = lax.broadcasted_iota(jnp.int32, (256, 256), 0) < lax.broadcasted_iota(jnp.int32, (256, 256), 1)
    counted_s = jnp.dot(dn.astype(BF), before.astype(F32).astype(BF), preferred_element_type=F32)[0:1]
    t = x * 64 + lax.broadcasted_iota(jnp.int32, (64, 256), 0)
    s = lax.broadcasted_iota(jnp.int32, (64, 256), 1)
    counted_t = jnp.sum(jnp.where(s < t, dn[0:1], 0.0), axis=1, keepdims=True)
    linked = (counted_t == counted_s) & (s >= t)
    powers = jnp.exp(jnp.maximum(s - t, 0).astype(F32) * math.log(GAMMA * LAMBDA))
    advantage = jnp.sum(jnp.where(linked, powers, 0.0) * deltas, axis=1, keepdims=True)
    own_old = jnp.sum(jnp.where(s == t, ov[0:1], 0.0), axis=1, keepdims=True)
    mask = jnp.where(t[:, 0:1] < lengths[y], 1.0, 0.0)
    return advantage + own_old, mask


STREAMS = ((True, 1), (True, -1), (False, 1), (False, -1))


def forward_kernel(feat, w4, down, head, rew, old, dones, lengths, bg, loss,
                   both, hid, part, rv1, rv2, og, mix,
                   s1, r1, s2, r2, gs1, gr1, gs2, gr2):
    x, y = lax.axis_index(X), lax.axis_index(Y)
    greet([{X: ring(x, 1)}, {X: ring(x, -1)}, {Y: ring(y, 1)}, {Y: ring(y, -1)}])

    def peer(first, h, delta):
        along_x = STREAMS[h][0] == first
        return {X: ring(x, delta)} if along_x else {Y: ring(y, delta)}

    def tok(h, da, db):
        dx, dy = (da, db) if STREAMS[h][0] else (db, da)
        return pl.ds(mul_of(ring(y, dy) * 256 + ring(x, dx) * 64, 64), 64)

    def offsets(h):
        s = STREAMS[h][1]
        return (2, s, -s, 0)

    one = {}
    two = {}
    for h in range(4):
        s = STREAMS[h][1]
        for j, db in enumerate(offsets(h)):
            for kind, (da, to) in enumerate(((2, s), (s, s), (-s, -s))):
                one[h, kind, j] = remote(part.at[h, tok(h, da, db)], rv1.at[h, kind, j],
                                         s1.at[h, kind, j], r1.at[h, kind, j], peer(True, h, to))
        for kind, (db, to) in enumerate(((2, s), (s, s), (-s, -s))):
            two[h, kind] = remote(part.at[h, tok(h, 0, db)], rv2.at[h, kind],
                                  s2.at[h, kind], r2.at[h, kind], peer(False, h, to))

    def chunk(dy):
        rows = pl.ds(mul_of(ring(y, dy) * 256, 256), 256)
        f = feat[rows, :]
        for c in range(4):
            gu = jnp.dot(f, w4[c], preferred_element_type=F32)
            both[c, rows, :] = gu
            gate, up = gu[:, :128], gu[:, 128:]
            hid[rows, c * 128:(c + 1) * 128] = (gate * jax.nn.sigmoid(gate) * up).astype(BF)
        v = hid[rows, :]
        for h in range(4):
            part[h, rows, :] = jnp.dot(
                v, down[:, h * 512:(h + 1) * 512], preferred_element_type=F32).astype(BF)

    def index(h, db):
        return offsets(h).index(db)

    def send_raw(dy):
        for h in (0, 1):
            one[h, 0, index(h, dy)].start()
            one[h, 2, index(h, dy)].start()
        for h in (2, 3):
            s = STREAMS[h][1]
            if dy == 2:
                for j in range(4):
                    one[h, 0, j].start()
            elif dy == -s:
                for j in range(4):
                    one[h, 2, j].start()

    def pass_on(h, j):
        s = STREAMS[h][1]
        one[h, 0, j].wait_recv()
        t = tok(h, s, offsets(h)[j])
        part[h, t, :] = (part[h, t, :].astype(F32) + rv1[h, 0, j].astype(F32)).astype(BF)
        one[h, 1, j].start()

    def finish(h, j):
        one[h, 1, j].wait_recv()
        one[h, 2, j].wait_recv()
        t = tok(h, 0, offsets(h)[j])
        total = part[h, t, :].astype(F32) + rv1[h, 1, j].astype(F32) + rv1[h, 2, j].astype(F32)
        if j == 3:
            two[h, 1].wait_recv()
            two[h, 2].wait_recv()
            mix[:, h * 512:(h + 1) * 512] = total + rv2[h, 1].astype(F32) + rv2[h, 2].astype(F32)
            return
        if j == 1:
            two[h, 0].wait_recv()
            total = total + rv2[h, 0].astype(F32)
        part[h, t, :] = total.astype(BF)
        two[h, j].start()

    chunk(2)
    send_raw(2)
    chunk(1)
    send_raw(1)
    for h in (0, 1):
        pass_on(h, index(h, 2))
    for j in range(4):
        pass_on(2, j)
    chunk(-1)
    send_raw(-1)
    for h in (0, 1):
        pass_on(h, index(h, 1))
    for j in range(4):
        pass_on(3, j)
    chunk(0)
    send_raw(0)
    for h in (0, 1):
        pass_on(h, index(h, -1))
    targets, mask = own_targets(x, y, rew, old, dones, lengths)
    for h in range(4):
        finish(h, 0)
    for h in (0, 1):
        pass_on(h, index(h, 0))
    for j in (1, 2, 3):
        for h in range(4):
            finish(h, j)

    mine = pl.ds(mul_of(y * 256 + x * 64, 64), 64)
    stream = feat[mine, :].astype(F32) + mix[...]
    vh = head[...]
    norm = lax.rsqrt(jnp.sum(stream * stream, axis=1, keepdims=True) / D + 1e-05)
    estimate = norm * jnp.sum(stream * vh, axis=1, keepdims=True)
    errors = estimate - targets
    total_tokens = TOK * 8
    loss[...] = jnp.broadcast_to(jnp.sum(mask * errors * errors, axis=0, keepdims=True) / total_tokens, (8, 128))
    coeff = 2.0 * mask * errors / total_tokens
    inner = coeff * estimate / D
    a = norm * coeff
    b = norm * norm * inner
    for h in range(4):
        cols = slice(h * 512, (h + 1) * 512)
        st = feat[mine, cols].astype(F32) + mix[:, cols]
        og[h, mine, :] = (a * vh[:, cols] - b * st).astype(BF)

    g1 = {}
    g2 = {}
    for h in range(4):
        s = STREAMS[h][1]
        for kind, (db, to) in enumerate(((0, 1), (0, -1), (-s, s))):
            t = og.at[h, tok(h, 0, db)]
            g1[h, kind] = remote(t, t, gs1.at[h, kind], gr1.at[h, kind], peer(False, h, to))
        for k, db in enumerate((0, -s, s, 2)):
            for kind, (da, to) in enumerate(((0, 1), (0, -1), (-s, s))):
                t = og.at[h, tok(h, da, db)]
                g2[h, k, kind] = remote(t, t, gs2.at[h, k, kind], gr2.at[h, k, kind], peer(True, h, to))

    waited = set()

    def arrive(table, key):
        if (id(table), key) not in waited:
            waited.add((id(table), key))
            table[key].wait_recv()

    def spread(h, k):
        g2[h, k, 0].start()
        g2[h, k, 1].start()

    def relay(h, k):
        kind = 0 if STREAMS[h][1] == 1 else 1
        arrive(g2, (h, k, kind))
        g2[h, k, 2].start()

    def backward(dy):
        rows = pl.ds(mul_of(ring(y, dy) * 256, 256), 256)
        hg = None
        for h in range(4):
            term = lax.dot_general(og[h, rows, :], down[:, h * 512:(h + 1) * 512],
                                   (((1,), (1,)), ((), ())), preferred_element_type=F32)
            hg = term if hg is None else hg + term
        for c in range(4):
            gate, up = both[c, rows, :128], both[c, rows, 128:]
            d = hg[:, c * 128:(c + 1) * 128]
            sig = jax.nn.sigmoid(gate)
            bg[rows, c * 256:c * 256 + 128] = (d * up * sig * (1.0 + gate * (1.0 - sig))).astype(BF)
            bg[rows, c * 256 + 128:(c + 1) * 256] = (d * gate * sig).astype(BF)

    for h in range(4):
        g1[h, 0].start()
        g1[h, 1].start()
    for h in range(4):
        spread(h, 0)
    for h in range(4):
        with_relay, against = (0, 1) if STREAMS[h][1] == 1 else (1, 0)
        arrive(g1, (h, with_relay))
        g1[h, 2].start()
    for h in range(4):
        spread(h, 1)
    for h in range(4):
        relay(h, 0)
        arrive(g1, (h, 1 if STREAMS[h][1] == 1 else 0))
        spread(h, 2)
    for h in range(4):
        arrive(g1, (h, 2))
        spread(h, 3)
    for h in range(4):
        relay(h, 1)
    for h in (0, 1):
        for kind in range(3):
            arrive(g2, (h, 0, kind))
    backward(0)
    for h in range(4):
        relay(h, 2)
    for dy in (-1, 1):
        for h in (0, 1):
            k = (0, -STREAMS[h][1], STREAMS[h][1], 2).index(dy)
            for kind in range(3):
                arrive(g2, (h, k, kind))
        for h in (2, 3):
            for k in range(4):
                arrive(g2, (h, k, 0 if dy == -1 else 1))
        if dy == -1:
            for h in range(4):
                relay(h, 3)
        backward(dy)
    for h in range(4):
        for k in range(4):
            for kind in range(3):
                arrive(g2, (h, k, kind))
    backward(2)

    for table in (one, two, g1, g2):
        for key in table:
            table[key].wait_send()


def update_kernel(feat, bg, loss_in, master, moment, second, work, master_new, moment_new, second_new, loss,
                  gsend, gown, grecv, qs, qr, gv, wk, mo, vo, so, n1, n2,
                  ds, dr, zs, zr, ns, nr, ms, mr, ws, wr, cs, cr, ls):
    z, core, x, y = (lax.axis_index(a) for a in (Z, CORE, X, Y))
    other = 1 - core
    me = z * 2 + core
    plane = x * 4 + y
    dp_peers = [{Z: ring(z, i // 2), CORE: lax.rem(core + i % 2, 2)} for i in range(1, 8)]
    mp_peers = [{X: ring(x, i // 4), Y: ring(y, i % 4)} for i in range(1, 16)]
    greet(dp_peers + mp_peers)

    order = (2, 1, -1, 0)
    swap = [remote(gsend.at[i], grecv.at[i], ds.at[i], dr.at[i], {CORE: other}) for i in range(4)]

    def grad_rows(dz, c):
        cols = pl.ds(mul_of((ring(z, dz) * 2 + c) * ROWS, ROWS), ROWS)
        return lax.dot_general(feat[:, cols], bg[...], (((0,), (0,)), ((), ())), preferred_element_type=F32)

    hop = {}
    for h, s in enumerate((1, -1)):
        for kind, to in enumerate((s, s, -s)):
            for j in range(4):
                rows = pl.ds(0, 80) if j == 0 else pl.ds(16 + 64 * j, 64)
                hop[h, kind, j] = remote(qs.at[h, kind, rows], qr.at[h, kind, rows],
                                         zs.at[h, kind, j], zr.at[h, kind, j], {Z: ring(z, to)})

    def exponent_of(bound):
        return jnp.ceil(4.0 * jnp.log2(jnp.maximum(bound, 1e-30)) + 0.02)

    def power(exponent):
        return jnp.exp(exponent * (math.log(2.0) / 4.0))

    def received(h, kind):
        exponent = qr[h, kind, 0:16, :].astype(jnp.int32).astype(F32)[0:1]
        return power(exponent)

    def head_of(h, kind, bound):
        exponent = exponent_of(bound)
        qs[h, kind, 0:16, :] = jnp.broadcast_to(exponent, (16, 512)).astype(jnp.int32).astype(jnp.int16)
        return LEVELS * power(-exponent)

    def both_cores(i, h):
        cols = slice(512 * h, 512 * (h + 1))
        size = jnp.zeros((8, 512), F32)
        for j in range(4):
            rows = slice(64 * j, 64 * (j + 1))
            t = gown[i, rows, cols] + grecv[i, rows, cols]
            gown[i, rows, cols] = t
            size = jnp.maximum(size, jnp.max(jnp.abs(t).reshape(8, 8, 512), axis=0))
        return jnp.max(size, axis=0, keepdims=True)

    def own(i, h, j):
        return gown[i, 64 * j:64 * (j + 1), 512 * h:512 * (h + 1)]

    def code(value, scale):
        return jnp.round(value * scale).astype(jnp.int32).astype(jnp.int16)

    def value_of(h, kind, j, unit):
        return qr[h, kind, 16 + 64 * j:80 + 64 * j, :].astype(jnp.int32).astype(F32) * unit

    def straight(i, h, kind):
        scale = head_of(h, kind, both_cores(i, h))
        for j in range(4):
            qs[h, kind, 16 + 64 * j:80 + 64 * j, :] = code(own(i, h, j), scale)
            hop[h, kind, j].start()

    def pass_on(i, h):
        size = both_cores(i, h)
        hop[h, 0, 0].wait_recv()
        far_size = received(h, 0)
        scale = head_of(h, 1, size + far_size)
        for j in range(4):
            if j > 0:
                hop[h, 0, j].wait_recv()
            qs[h, 1, 16 + 64 * j:80 + 64 * j, :] = code(own(i, h, j) + value_of(h, 0, j, far_size / LEVELS), scale)
            hop[h, 1, j].start()

    for i, dz in enumerate(order):
        gsend[i] = grad_rows(dz, other)
        swap[i].start()
        gown[i] = grad_rows(dz, core)
        if i == 1:
            swap[0].wait_recv()
            straight(0, 0, 0)
            straight(0, 1, 0)
        if i == 2:
            swap[1].wait_recv()
            straight(1, 1, 2)
        if i == 3:
            swap[2].wait_recv()
            straight(2, 0, 2)
    pass_on(1, 0)
    pass_on(2, 1)
    swap[3].wait_recv()
    squares = jnp.zeros((8, 128), F32)
    units = {}
    for j in range(4):
        for h in range(2):
            hop[h, 2, j].wait_recv()
            hop[h, 1, j].wait_recv()
            if j == 0:
                units[h] = [received(h, kind) / LEVELS for kind in (1, 2)]
            part = gown[3, 64 * j:64 * (j + 1), 512 * h:512 * (h + 1)] + grecv[3, 64 * j:64 * (j + 1), 512 * h:512 * (h + 1)]
            g = part + value_of(h, 1, j, units[h][0]) + value_of(h, 2, j, units[h][1])
            for c in range(4):
                piece = g[:, c * 128:(c + 1) * 128]
                gv[pl.ds(64 * j * 8 + 4 * h + c, 64, stride=8), :] = piece
                squares = squares + jnp.sum((piece * piece).reshape(8, 8, 128), axis=0)

    n1[me, 0:8, :] = squares
    n1[me, 8:16, :] = loss_in[...]
    near = [remote(n1.at[me], n1.at[me], ns.at[i], nr.at[i], p) for i, p in enumerate(dp_peers)]
    for c in near:
        c.start()
    for c in near:
        c.wait_recv()
    sums = n1[0]
    for i in range(1, 8):
        sums = sums + n1[i]
    n2[plane] = sums
    far = [remote(n2.at[plane], n2.at[plane], ms.at[i], mr.at[i], p) for i, p in enumerate(mp_peers)]
    for c in far:
        c.start()
    for c in far:
        c.wait_recv()
    sums = n2[0]
    for i in range(1, 16):
        sums = sums + n2[i]
    loss[...] = sums[8:16]
    squared = jnp.sum(jnp.sum(sums[0:8], axis=1, keepdims=True), axis=0, keepdims=True)
    clip = jnp.minimum(1.0, MAX_NORM / (jnp.sqrt(squared) + 1e-06))

    def place(device, q):
        return pl.ds(mul_of(device * 2048 + q * 256, 256), 256)

    def block(device, q):
        return wk.at[place(device, q)]

    spread = {}
    for q in range(8):
        s = 1 if q % 2 == 0 else -1
        src = {0: (me, {Z: ring(z, 1)}), 1: (me, {Z: ring(z, -1)}),
               2: (ring(z, -s) * 2 + core, {Z: ring(z, s)}),
               3: (me, {CORE: other}), 4: (ring(z, -1) * 2 + core, {CORE: other}),
               5: (ring(z, 1) * 2 + core, {CORE: other}), 6: (ring(z, 2) * 2 + core, {CORE: other})}
        for kind, (device, to) in src.items():
            b = block(device, q)
            spread[q, kind] = remote(b, b, ws.at[q, kind], wr.at[q, kind], to)
    for q in range(8):
        rows = pl.ds(256 * q, 256)
        g = gv[rows, :] * clip
        m = 0.9 * moment[rows, :] + 0.1 * g
        v = 0.999 * second[rows, :] + 0.001 * g * g
        old = master[rows, :]
        first_hat = m * (1.0 / (1.0 - 0.9 ** 10))
        second_hat = v * (1.0 / (1.0 - 0.999 ** 10))
        new = old - 0.001 * (first_hat / (jnp.sqrt(second_hat) + 1e-08) + 0.1 * old)
        mo[rows, :] = new
        vo[rows, :] = m
        so[rows, :] = v
        wk[place(me, q), :] = new.astype(BF)
        for kind in (0, 1, 3):
            spread[q, kind].start()
    local = [pltpu.make_async_copy(a, b, ls.at[i])
             for i, (a, b) in enumerate(((mo, master_new), (vo, moment_new), (so, second_new)))]
    for c in local:
        c.start()
    for q in range(8):
        with_relay, against = (0, 1) if q % 2 == 0 else (1, 0)
        spread[q, with_relay].wait_recv()
        spread[q, 2].start()
        spread[q, 4 + with_relay].start()
        spread[q, against].wait_recv()
        spread[q, 4 + against].start()
    out = {}

    def store(i, device):
        rows = pl.ds(mul_of(device * 2048, 2048), 2048)
        out[i] = pltpu.make_async_copy(wk.at[rows], work.at[rows], cs.at[i])
        out[i].start()

    store(0, me)
    store(1, ring(z, 1) * 2 + core)
    store(2, ring(z, -1) * 2 + core)
    for q in range(8):
        spread[q, 2].wait_recv()
        spread[q, 6].start()
    store(3, ring(z, 2) * 2 + core)
    for i, kind in enumerate((3, 4, 5, 6)):
        for q in range(8):
            spread[q, kind].wait_recv()
        store(4 + i, ring(z, (0, -1, 1, 2)[i]) * 2 + other)
    for c in local:
        c.wait()
    for i in out:
        out[i].wait()
    for c in swap + near + far:
        c.wait_send()
    for table in (hop, spread):
        for key in table:
            table[key].wait_send()


def rows_of(value):
    r = value.shape[0]
    return value.reshape(r, 2, 4, 128).transpose(0, 2, 1, 3).reshape(r * 8, 128)


def from_rows(value):
    r = value.shape[0] // 8
    return value.reshape(r, 4, 2, 128).transpose(0, 2, 1, 3).reshape(r, 2, 512)


def per_device(features, rewards, old_values, dones, lengths, proj_weights, down_weight, value_head,
               master, moment, second):
    dma = pltpu.SemaphoreType.DMA
    vm = pl.BlockSpec(memory_space=pltpu.VMEM)
    sm = pl.BlockSpec(memory_space=pltpu.SMEM)
    anyspace = pl.BlockSpec(memory_space=pl.ANY)
    w4 = proj_weights.reshape(D, 2, 4, 128).transpose(2, 0, 1, 3).reshape(4, D, 256)
    bg, loss_part = pl.pallas_call(
        forward_kernel,
        name="forward_and_backward",
        out_shape=(jax.ShapeDtypeStruct((TOK, 2 * FFL), BF), jax.ShapeDtypeStruct((8, 128), F32)),
        in_specs=[vm] * 7 + [sm],
        out_specs=(vm, vm),
        scratch_shapes=[
            pltpu.VMEM((4, TOK, 256), F32), pltpu.VMEM((TOK, FFL), BF), pltpu.VMEM((4, TOK, 512), BF),
            pltpu.VMEM((4, 3, 4, 64, 512), BF), pltpu.VMEM((4, 3, 64, 512), BF), pltpu.VMEM((4, TOK, 512), BF),
            pltpu.VMEM((64, D), F32),
            dma((4, 3, 4)), dma((4, 3, 4)), dma((4, 3)), dma((4, 3)),
            dma((4, 3)), dma((4, 3)), dma((4, 4, 3)), dma((4, 4, 3)),
        ],
        compiler_params=pltpu.CompilerParams(collective_id=0, has_side_effects=True, vmem_limit_bytes=VMEM_LIMIT),
    )(features, w4, down_weight, value_head.reshape(1, D), rewards, old_values, dones, lengths)
    rows = jax.ShapeDtypeStruct((8 * ROWS, 128), F32)
    work, master_new, moment_new, second_new, loss = pl.pallas_call(
        update_kernel,
        name="gradients_and_update",
        out_shape=(jax.ShapeDtypeStruct((8 * D, 128), BF), rows, rows, rows, jax.ShapeDtypeStruct((8, 128), F32)),
        in_specs=[vm] * 6,
        out_specs=(anyspace, anyspace, anyspace, anyspace, vm),
        scratch_shapes=[
            pltpu.VMEM((4, ROWS, 1024), F32), pltpu.VMEM((4, ROWS, 1024), F32), pltpu.VMEM((4, ROWS, 1024), F32),
            pltpu.VMEM((2, 3, 16 + ROWS, 512), jnp.int16), pltpu.VMEM((2, 3, 16 + ROWS, 512), jnp.int16),
            pltpu.VMEM((8 * ROWS, 128), F32), pltpu.VMEM((8 * D, 128), BF),
            pltpu.VMEM((8 * ROWS, 128), F32), pltpu.VMEM((8 * ROWS, 128), F32), pltpu.VMEM((8 * ROWS, 128), F32),
            pltpu.VMEM((8, 16, 128), F32), pltpu.VMEM((16, 16, 128), F32),
            dma((4,)), dma((4,)), dma((2, 3, 4)), dma((2, 3, 4)), dma((7,)), dma((7,)), dma((15,)), dma((15,)),
            dma((8, 7)), dma((8, 7)), dma((8,)), dma((8,)), dma((3,)),
        ],
        compiler_params=pltpu.CompilerParams(collective_id=1, has_side_effects=True, vmem_limit_bytes=VMEM_LIMIT),
    )(features, bg, loss_part, rows_of(master), rows_of(moment), rows_of(second))
    return (from_rows(master_new), from_rows(moment_new), from_rows(second_new), from_rows(work), loss[0, 0])


def solution(mesh):
    finer = Mesh(mesh.devices.reshape(4, 2, 4, 4), (Z, CORE, X, Y))
    return jax.shard_map(
        per_device,
        mesh=finer,
        in_specs=(
            P(DP, None), P(DP, None), P(DP, None), P(DP, None), P(DP),
            P(None, None, MP), P(MP, None), P(),
            P(DP, None, MP), P(DP, None, MP), P(DP, None, MP),
        ),
        out_specs=(P(DP, None, MP), P(DP, None, MP), P(DP, None, MP), P(None, None, MP), P()),
        check_vma=False,
    )
```

time: 350 us -> 163 us (0.47)
  waiting for transfers between devices: 198 us -> 0 us
  Pallas kernels: 0 us -> 135 us
  matrix products: 33.5 us -> 0 us
  blocking collectives: 30.7 us -> 0 us
  local copies, waits for them, and re-layouts: 55.1 us -> 26.3 us
  other arithmetic: 15.3 us -> 0 us
  between operations: 15.3 us -> 0.66 us
    pallas_call x0 -> x2, Pallas kernels: none -> 135 us  [the longest x1 72 us: per_device(): pl.pallas_call(update_kernel, name='gradients_and_update', out_shape=(jax...]
    psum x1 -> x0, waiting for transfers between devices: 103 us -> none  [per_device(): lax.psum(jnp.dot(hidden, down_weight, preferred_element_type=jnp.float32)...]
    reduce_scatter x2 -> x0, waiting for transfers between devices: 69.5 us -> none  [own_block(): parts = lax.psum_scatter(parts, axes[k], scatter_dimension=0, tiled=True)]
    dot_general x6 -> x0, matrix products: 33.5 us -> none  [the longest x1 8.13 us: value_loss(): estimate = jnp.dot(normed, value_head, precision=lax.Precision.HIGHEST)]
    psum x4 -> x0, blocking collectives: 30.7 us -> none  [one_axis_at_a_time(): return functools.reduce(lax.psum, axes, value)]
    all_gather x1 -> x0, waiting for transfers between devices: 26.3 us -> none  [per_device(): lax.all_gather(master_new.astype(jnp.bfloat16), DP, axis=0, tiled=True)]
    unnamed x28 -> x6, local copies, waits for them, and re-layouts: 22 us -> 9.68 us
    another operation x3 -> x0, local copies, waits for them, and re-layouts: 11.8 us -> none  [the longest x1 11.7 us: own_block(): parts = parts.reshape(*shape, *parts.shape[1:])]
  transfers between devices with their start and end apart: 4 -> 0, of which waited for: 4 -> 0; matrix products, arithmetic and copies ran while one was open for 2% -> 0% of each run, Pallas kernels for 0% -> 0%
where the time goes in v1:
time: 163 us; the launch traced here: 162 us
  Pallas kernels  135 us (83%)
  local copies, waits for them, and re-layouts  26.3 us (16%)
    pallas_call x1, Pallas kernels, per_device(): pl.pallas_call(update_kernel, name='gradients_and_update', out_shape=(jax...  72 us
    pallas_call x1, Pallas kernels, per_device(): pl.pallas_call(forward_kernel, name='forward_and_backward', out_shape=(ja...  63.3 us
    unnamed x6, local copies, waits for them, and re-layouts  9.68 us
    transpose x1, local copies, waits for them, and re-layouts, per_device(): proj_weights.reshape(D, 2, 4, 128).transpose(2, 0, 1, 3).reshape(4, D, 256)  7.71 us
    reshape x1, local copies, waits for them, and re-layouts, per_device(): proj_weights.reshape(D, 2, 4, 128).transpose(2, 0, 1, 3).reshape(4, D, 256)  7.59 us

profile of v1, /device:TPU:1, one launch (start us, length us, event | category | flops | bytes accessed | tf_op | source)
XLA Modules:
  0.0 162.3 jit_solution(4227657029335235894)
XLA Ops:
  0.6 7.7 %bitcast_bitcast_fusion = bf16[4,2048,2,128]{3,2,1,0:T(2,128)(2,1)} fusion(bf16[2048,2,512]{2,1,0:T(2,128)(2,1)} %param.16), kind=kLoop, calls=%fused_computation | loop fusion | bytes 8388608 | tf_op jit(solution)/shard_map/transpose | solution.py:508
  8.3 7.6 %reshape.62.w4 = bf16[4,2048,256]{2,1,0:T(8,128)(2,1)} reshape(bf16[4,2048,2,128]{3,2,1,0:T(2,128)(2,1)} %bitcast_bitcast_fusion) | data formatting | bytes 8388608 | tf_op jit(solution)/shard_map/reshape | solution.py:508
  15.9 63.3 %forward_and_backward.1 = (bf16[1024,1024]{1,0:T(8,128)(2,1)}, f32[8,128]{1,0:T(8,128)}) custom-call(bf16[1024,2048]{1,0:T(8,128)(2,1)} %feat.3, bf16[4,2048,256]{2,1,0:T(8,128)(2,1)} %reshape.62.w4, bf16[512,2048]{1,0:T(8,128)(2,1)} %down.1, f32[1,2048]{1,0:T(1,128)} %bitcast.51, f32[4,256]{1,0:T(4,128)} %rew.1, f32[4,256]{1,0:T(4,128)} %old.1, ...), custom_call_target="tpu_custom_call" | custom-call | tf_op jit(solution)/shard_map/forward_and_backward/pallas_call | solution.py:509
  79.2 72.0 %gradients_and_update.1 = (bf16[16384,128]{1,0:T(8,128)(2,1)}, f32[2048,128]{1,0:T(8,128)}, f32[2048,128]{1,0:T(8,128)}, f32[2048,128]{1,0:T(8,128)}, f32[8,128]{1,0:T(8,128)}) custom-call(bf16[1024,2048]{1,0:T(8,128)(2,1)} %feat.3, bf16[1024,1024]{1,0:T(8,128)(2,1)} %get-tuple-element.12.bg, f32[8,128]{1,0:T(8,128)} %get-tuple-element.13.loss_in, ...), custom_call_target="tpu_custom_call" | custom-call | tf_op jit(solution)/shard_map/gradients_and_update/pallas_call | solution.py:525
  151.2 0.0 copy-start
  151.2 1.3 slice.3
  152.6 2.6 %copy.30 = f32[256,2,512]{2,1,0:T(2,128)} copy(f32[256,2,512]{2,1,0:T(2,128)} %bitcast.50) | data formatting | bytes 2097152
  155.1 2.6 %copy.31 = f32[256,2,512]{2,1,0:T(2,128)} copy(f32[256,2,512]{2,1,0:T(2,128)} %bitcast.49) | data formatting | bytes 2097152
  157.7 2.6 %copy.32 = f32[256,2,512]{2,1,0:T(2,128)} copy(f32[256,2,512]{2,1,0:T(2,128)} %bitcast.48) | data formatting | bytes 2097152
  160.2 0.0 copy-done
  160.2 2.0 %copy.33 = bf16[2048,2,512]{2,1,0:T(2,128)(2,1)} copy(bf16[2048,2,512]{2,1,0:T(2,128)(2,1)S(1)} %bitcast.44) | data formatting | bytes 8388608
Async XLA Ops:
  151.2 9.0 %copy-start = (bf16[16384,128]{1,0:T(8,128)(2,1)S(1)}, bf16[16384,128]{1,0:T(8,128)(2,1)}, u32[]{:S(2)}) copy-start(bf16[16384,128]{1,0:T(8,128)(2,1)} %get-tuple-element.17) | copy-start | bytes 12582916

commit v2 on v1

v2 whole, which is shorter than its diff:
```python
import math

import jax
import jax.numpy as jnp
from jax import lax
from jax.experimental import pallas as pl
from jax.experimental.pallas import tpu as pltpu
from jax.sharding import Mesh
from jax.sharding import PartitionSpec as P

Z, CORE, X, Y = "dp_0", "dp_1", "mp_0", "mp_1"
DP = (Z, CORE)
MP = (X, Y)
GAMMA = 0.99
LAMBDA = 0.95
MAX_NORM = 0.05
D = 2048
TOK = 1024
FFL = 512
ROWS = 256
BF = jnp.bfloat16
LEVELS = 32000.0
F32 = jnp.float32
VMEM_LIMIT = 62 * 1024 * 1024


def mul_of(v, n):
    return pl.multiple_of(v, n)


def ring(v, d):
    return lax.rem(v + (d + 4), 4)


def remote(src, dst, send, recv, device):
    return pltpu.make_async_remote_copy(
        src_ref=src, dst_ref=dst, send_sem=send, recv_sem=recv,
        device_id=device, device_id_type=pl.DeviceIdType.MESH,
    )


def greet(devices):
    barrier = pltpu.get_barrier_semaphore()
    for device in devices:
        pl.semaphore_signal(barrier, inc=1, device_id=device, device_id_type=pl.DeviceIdType.MESH)
    pl.semaphore_wait(barrier, len(devices))


def own_targets(row, start, rew, old, dones, lengths):
    dn = jnp.broadcast_to(dones[pl.ds(row, 1), :].astype(F32), (8, 256))
    ov = jnp.broadcast_to(old[pl.ds(row, 1), :], (8, 256))
    rw = jnp.broadcast_to(rew[pl.ds(row, 1), :], (8, 256))
    lane = lax.broadcasted_iota(jnp.int32, (8, 256), 1)
    following = jnp.where(lane == 255, 0.0, pltpu.roll(ov, 255, axis=1))
    deltas = (rw + GAMMA * following * (1.0 - dn) - ov)[0:1]
    before = lax.broadcasted_iota(jnp.int32, (256, 256), 0) < lax.broadcasted_iota(jnp.int32, (256, 256), 1)
    counted_s = jnp.dot(dn.astype(BF), before.astype(F32).astype(BF), preferred_element_type=F32)[0:1]
    t = start + lax.broadcasted_iota(jnp.int32, (WT, 256), 0)
    s = lax.broadcasted_iota(jnp.int32, (WT, 256), 1)
    counted_t = jnp.sum(jnp.where(s < t, dn[0:1], 0.0), axis=1, keepdims=True)
    linked = (counted_t == counted_s) & (s >= t)
    powers = jnp.exp(jnp.maximum(s - t, 0).astype(F32) * math.log(GAMMA * LAMBDA))
    advantage = jnp.sum(jnp.where(linked, powers, 0.0) * deltas, axis=1, keepdims=True)
    own_old = jnp.sum(jnp.where(s == t, ov[0:1], 0.0), axis=1, keepdims=True)
    mask = jnp.where(t[:, 0:1] < lengths[row], 1.0, 0.0)
    return advantage + own_old, mask


STREAMS = ((True, 1), (True, -1), (False, 1), (False, -1))
WT = 32
WAVE = 512


def step_kernel(feat_hbm, w_hbm, down_hbm, master_hbm, moment_hbm, second_hbm, head, rew, old, dones, lengths,
                work, grad_out, sums_out,
                feat, w4, down, both, hid, part, rv1, rv2, og, mix, bg,
                master, moment, second, gsend, gown, grecv, qs, qr, gv, wk, n1, n2,
                fs, rs, os, s1, r1, s2, r2, gs1, gr1, gs2, gr2,
                ds, dr, zs, zr, ns, nr, ms, mr, ws, wr, cs, ls):
    z, core, x, y = (lax.axis_index(a) for a in (Z, CORE, X, Y))
    other = 1 - core
    me = z * 2 + core
    plane = x * 4 + y
    dp_peers = [{Z: ring(z, i // 2), CORE: lax.rem(core + i % 2, 2)} for i in range(1, 8)]
    mp_peers = [{X: ring(x, i // 4), Y: ring(y, i % 4)} for i in range(1, 16)]

    load_w = []
    for p in range(4):
        rows = pl.ds(4096 * p, 4096)
        load_w.append(pltpu.make_async_copy(w_hbm.at[rows], wk.at[rows], rs.at[p]))
        load_w[p].start()
    load_f = {}
    for w in range(2):
        for i, dy in enumerate((2, 1, -1, 0)):
            rows = pl.ds(mul_of(ring(y, dy) * 128 + WAVE * w, 128), 128)
            load_f[w, dy] = pltpu.make_async_copy(feat_hbm.at[rows], feat.at[rows], fs.at[w, i])
    load_d = pltpu.make_async_copy(down_hbm, down, os.at[0])
    load_f[0, 2].start()
    load_d.start()
    for key in load_f:
        if key != (0, 2):
            load_f[key].start()
    state = [pltpu.make_async_copy(a, b, os.at[i]) for i, a, b in
             ((1, master_hbm, master), (2, moment_hbm, moment), (3, second_hbm, second))]
    for c in state:
        c.start()
    greet(dp_peers + mp_peers)

    out_row = lax.broadcasted_iota(jnp.int32, (256, 256), 0)
    in_row = lax.broadcasted_iota(jnp.int32, (256, 256), 1)
    select = jnp.where(in_row == (out_row % 32) * 8 + out_row // 32, 1.0, 0.0).astype(BF)
    for p in range(4):
        load_w[p].wait()
        for u in range(8):
            base = 4096 * p + 512 * u
            pair = jnp.concatenate([wk[base:base + 256, :], wk[base + 256:base + 512, :]], axis=1)
            moved = jnp.dot(select, pair, preferred_element_type=F32).astype(BF)
            k = 512 * p + 64 * u
            for i in range(8):
                c, g = i // 2, i % 2
                for half in range(2):
                    w4[c, k + 32 * half:k + 32 * half + 32, 128 * g:128 * (g + 1)] = \
                        moved[32 * i:32 * (i + 1), 128 * half:128 * (half + 1)]
    load_d.wait()

    def peer(first, h, delta):
        along_x = STREAMS[h][0] == first
        return {X: ring(x, delta)} if along_x else {Y: ring(y, delta)}

    def tok(w, h, da, db):
        dx, dy = (da, db) if STREAMS[h][0] else (db, da)
        return pl.ds(mul_of(WAVE * w + ring(y, dy) * 128 + ring(x, dx) * WT, WT), WT)

    def offsets(h):
        s = STREAMS[h][1]
        return (2, s, -s, 0)

    def index(h, db):
        return offsets(h).index(db)

    one, two, g1, g2 = {}, {}, {}, {}
    for w in range(2):
        for h in range(4):
            s = STREAMS[h][1]
            for j, db in enumerate(offsets(h)):
                for kind, (da, to) in enumerate(((2, s), (s, s), (-s, -s))):
                    one[w, h, kind, j] = remote(part.at[h, tok(w, h, da, db)], rv1.at[w, h, kind, j],
                                                s1.at[w, h, kind, j], r1.at[w, h, kind, j], peer(True, h, to))
            for kind, (db, to) in enumerate(((2, s), (s, s), (-s, -s))):
                two[w, h, kind] = remote(part.at[h, tok(w, h, 0, db)], rv2.at[w, h, kind],
                                         s2.at[w, h, kind], r2.at[w, h, kind], peer(False, h, to))
            for kind, (db, to) in enumerate(((0, 1), (0, -1), (-s, s))):
                t = og.at[h, tok(w, h, 0, db)]
                g1[w, h, kind] = remote(t, t, gs1.at[w, h, kind], gr1.at[w, h, kind], peer(False, h, to))
            for k, db in enumerate((0, -s, s, 2)):
                for kind, (da, to) in enumerate(((0, 1), (0, -1), (-s, s))):
                    t = og.at[h, tok(w, h, da, db)]
                    g2[w, h, k, kind] = remote(t, t, gs2.at[w, h, k, kind], gr2.at[w, h, k, kind], peer(True, h, to))

    def chunk(w, dy):
        load_f[w, dy].wait()
        rows = pl.ds(mul_of(ring(y, dy) * 128 + WAVE * w, 128), 128)
        f = feat[rows, :]
        for c in range(4):
            gu = jnp.dot(f, w4[c], preferred_element_type=F32)
            both[c, rows, :] = gu
            gate, up = gu[:, :128], gu[:, 128:]
            hid[rows, c * 128:(c + 1) * 128] = (gate * jax.nn.sigmoid(gate) * up).astype(BF)
        v = hid[rows, :]
        for h in range(4):
            part[h, rows, :] = jnp.dot(
                v, down[:, h * 512:(h + 1) * 512], preferred_element_type=F32).astype(BF)
        for h in (0, 1):
            one[w, h, 0, index(h, dy)].start()
            one[w, h, 2, index(h, dy)].start()
        for h in (2, 3):
            s = STREAMS[h][1]
            if dy == 2:
                for j in range(4):
                    one[w, h, 0, j].start()
            elif dy == -s:
                for j in range(4):
                    one[w, h, 2, j].start()

    def pass_on(w, h, j):
        s = STREAMS[h][1]
        one[w, h, 0, j].wait_recv()
        t = tok(w, h, s, offsets(h)[j])
        part[h, t, :] = (part[h, t, :].astype(F32) + rv1[w, h, 0, j].astype(F32)).astype(BF)
        one[w, h, 1, j].start()

    def pass_x(w, dy):
        for h in (0, 1):
            pass_on(w, h, index(h, dy))

    def pass_y(w, h):
        for j in range(4):
            pass_on(w, h, j)

    def finish_one(w, h, j):
        one[w, h, 1, j].wait_recv()
        one[w, h, 2, j].wait_recv()
        t = tok(w, h, 0, offsets(h)[j])
        total = part[h, t, :].astype(F32) + rv1[w, h, 1, j].astype(F32) + rv1[w, h, 2, j].astype(F32)
        if j == 3:
            two[w, h, 1].wait_recv()
            two[w, h, 2].wait_recv()
            mix[w, :, h * 512:(h + 1) * 512] = total + rv2[w, h, 1].astype(F32) + rv2[w, h, 2].astype(F32)
            return
        if j == 1:
            two[w, h, 0].wait_recv()
            total = total + rv2[w, h, 0].astype(F32)
        part[h, t, :] = total.astype(BF)
        two[w, h, j].start()

    def finish(w, j):
        for h in range(4):
            finish_one(w, h, j)

    def own_loss(w, targets, mask):
        mine = pl.ds(mul_of(WAVE * w + y * 128 + x * WT, WT), WT)
        stream = feat[mine, :].astype(F32) + mix[w]
        vh = head[...]
        norm = lax.rsqrt(jnp.sum(stream * stream, axis=1, keepdims=True) / D + 1e-05)
        estimate = norm * jnp.sum(stream * vh, axis=1, keepdims=True)
        errors = estimate - targets
        total_tokens = TOK * 8
        coeff = 2.0 * mask * errors / total_tokens
        inner = coeff * estimate / D
        a = norm * coeff
        b = norm * norm * inner
        for h in range(4):
            cols = slice(h * 512, (h + 1) * 512)
            og[h, mine, :] = (a * vh[:, cols] - b * stream[:, cols]).astype(BF)
        return jnp.sum(mask * errors * errors, axis=0, keepdims=True) / total_tokens

    waited = set()

    def arrive(name, key):
        if (name, key) not in waited:
            waited.add((name, key))
            {"g1": g1, "g2": g2}[name][key].wait_recv()

    def ahead(h):
        return 0 if STREAMS[h][1] == 1 else 1

    def spread(w, h, k):
        g2[w, h, k, 0].start()
        g2[w, h, k, 1].start()

    def relay(w, k):
        for h in range(4):
            arrive("g2", (w, h, k, ahead(h)))
            g2[w, h, k, 2].start()

    def gather_0(w):
        for h in range(4):
            g1[w, h, 0].start()
            g1[w, h, 1].start()
        for h in range(4):
            spread(w, h, 0)

    def gather_1(w):
        for h in range(4):
            arrive("g1", (w, h, ahead(h)))
            g1[w, h, 2].start()
            spread(w, h, 1)

    def gather_2(w):
        relay(w, 0)
        for h in range(4):
            arrive("g1", (w, h, 1 - ahead(h)))
            spread(w, h, 2)

    def gather_3(w):
        for h in range(4):
            arrive("g1", (w, h, 2))
            spread(w, h, 3)

    def backward(w, dy):
        for h in (0, 1):
            k = (0, -STREAMS[h][1], STREAMS[h][1], 2).index(dy)
            for kind in range(3):
                arrive("g2", (w, h, k, kind))
        if dy != 0:
            for h in (2, 3):
                for k in range(4):
                    arrive("g2", (w, h, k, {-1: 0, 1: 1, 2: 2}[dy]))
        rows = pl.ds(mul_of(ring(y, dy) * 128 + WAVE * w, 128), 128)
        hg = None
        for h in range(4):
            term = lax.dot_general(og[h, rows, :], down[:, h * 512:(h + 1) * 512],
                                   (((1,), (1,)), ((), ())), preferred_element_type=F32)
            hg = term if hg is None else hg + term
        for c in range(4):
            gate, up = both[c, rows, :128], both[c, rows, 128:]
            d = hg[:, c * 128:(c + 1) * 128]
            sig = jax.nn.sigmoid(gate)
            bg[rows, c * 256:c * 256 + 128] = (d * up * sig * (1.0 + gate * (1.0 - sig))).astype(BF)
            bg[rows, c * 256 + 128:(c + 1) * 256] = (d * gate * sig).astype(BF)

    chunk(0, 2)
    chunk(0, 1)
    pass_x(0, 2)
    pass_y(0, 2)
    chunk(0, -1)
    pass_x(0, 1)
    pass_y(0, 3)
    chunk(0, 0)
    pass_x(0, -1)
    chunk(1, 2)
    own = [own_targets(2 * w + y // 2, (y % 2) * 128 + x * WT, rew, old, dones, lengths) for w in range(2)]
    finish(0, 0)
    pass_x(0, 0)
    chunk(1, 1)
    finish(0, 1)
    pass_x(1, 2)
    pass_y(1, 2)
    chunk(1, -1)
    finish(0, 2)
    pass_x(1, 1)
    finish(0, 3)
    loss = own_loss(0, *own[0])
    gather_0(0)
    pass_y(1, 3)
    chunk(1, 0)
    pass_x(1, -1)
    finish(1, 0)
    pass_x(1, 0)
    gather_1(0)
    finish(1, 1)
    gather_2(0)
    finish(1, 2)
    finish(1, 3)
    loss = loss + own_loss(1, *own[1])
    gather_0(1)
    gather_3(0)
    relay(0, 1)
    gather_1(1)
    relay(0, 2)
    relay(0, 3)
    gather_2(1)
    backward(0, 0)
    gather_3(1)
    backward(0, -1)
    relay(1, 1)
    backward(0, 1)
    relay(1, 2)
    backward(0, 2)
    relay(1, 3)
    for dy in (0, -1, 1, 2):
        backward(1, dy)

    order = (2, 1, -1, 0)
    swap = [remote(gsend.at[i], grecv.at[i], ds.at[i], dr.at[i], {CORE: other}) for i in range(4)]

    def grad_rows(dz, c):
        cols = pl.ds(mul_of((ring(z, dz) * 2 + c) * ROWS, ROWS), ROWS)
        return lax.dot_general(feat[:, cols], bg[...], (((0,), (0,)), ((), ())), preferred_element_type=F32)

    hop = {}
    for h, s in enumerate((1, -1)):
        for kind, to in enumerate((s, s, -s)):
            for j in range(4):
                rows = pl.ds(0, 80) if j == 0 else pl.ds(16 + 64 * j, 64)
                hop[h, kind, j] = remote(qs.at[h, kind, rows], qr.at[h, kind, rows],
                                         zs.at[h, kind, j], zr.at[h, kind, j], {Z: ring(z, to)})

    def exponent_of(bound):
        return jnp.ceil(4.0 * jnp.log2(jnp.maximum(bound, 1e-30)) + 0.02)

    def power(exponent):
        return jnp.exp(exponent * (math.log(2.0) / 4.0))

    def received(h, kind):
        exponent = qr[h, kind, 0:16, :].astype(jnp.int32).astype(F32)[0:1]
        return power(exponent)

    def head_of(h, kind, bound):
        exponent = exponent_of(bound)
        qs[h, kind, 0:16, :] = jnp.broadcast_to(exponent, (16, 512)).astype(jnp.int32).astype(jnp.int16)
        return LEVELS * power(-exponent)

    def both_cores(i, h):
        cols = slice(512 * h, 512 * (h + 1))
        size = jnp.zeros((8, 512), F32)
        for j in range(4):
            rows = slice(64 * j, 64 * (j + 1))
            t = gown[i, rows, cols] + grecv[i, rows, cols]
            gown[i, rows, cols] = t
            size = jnp.maximum(size, jnp.max(jnp.abs(t).reshape(8, 8, 512), axis=0))
        return jnp.max(size, axis=0, keepdims=True)

    def mine_of(i, h, j):
        return gown[i, 64 * j:64 * (j + 1), 512 * h:512 * (h + 1)]

    def code(value, scale):
        return jnp.round(value * scale).astype(jnp.int32).astype(jnp.int16)

    def value_of(h, kind, j, unit):
        return qr[h, kind, 16 + 64 * j:80 + 64 * j, :].astype(jnp.int32).astype(F32) * unit

    def straight(i, h, kind):
        scale = head_of(h, kind, both_cores(i, h))
        for j in range(4):
            qs[h, kind, 16 + 64 * j:80 + 64 * j, :] = code(mine_of(i, h, j), scale)
            hop[h, kind, j].start()

    def pass_sum(i, h):
        size = both_cores(i, h)
        hop[h, 0, 0].wait_recv()
        far_size = received(h, 0)
        scale = head_of(h, 1, size + far_size)
        for j in range(4):
            if j > 0:
                hop[h, 0, j].wait_recv()
            qs[h, 1, 16 + 64 * j:80 + 64 * j, :] = code(mine_of(i, h, j) + value_of(h, 0, j, far_size / LEVELS), scale)
            hop[h, 1, j].start()

    for i, dz in enumerate(order):
        gsend[i] = grad_rows(dz, other)
        swap[i].start()
        gown[i] = grad_rows(dz, core)
        if i == 1:
            swap[0].wait_recv()
            straight(0, 0, 0)
            straight(0, 1, 0)
        if i == 2:
            swap[1].wait_recv()
            straight(1, 1, 2)
        if i == 3:
            swap[2].wait_recv()
            straight(2, 0, 2)
    pass_sum(1, 0)
    pass_sum(2, 1)
    swap[3].wait_recv()
    squares = jnp.zeros((8, 128), F32)
    units = {}
    for j in range(4):
        for h in range(2):
            hop[h, 2, j].wait_recv()
            hop[h, 1, j].wait_recv()
            if j == 0:
                units[h] = [received(h, kind) / LEVELS for kind in (1, 2)]
            owned = gown[3, 64 * j:64 * (j + 1), 512 * h:512 * (h + 1)] + grecv[3, 64 * j:64 * (j + 1), 512 * h:512 * (h + 1)]
            g = owned + value_of(h, 1, j, units[h][0]) + value_of(h, 2, j, units[h][1])
            for c in range(4):
                piece = g[:, c * 128:(c + 1) * 128]
                gv[pl.ds(64 * j * 8 + 4 * h + c, 64, stride=8), :] = piece
                squares = squares + jnp.sum((piece * piece).reshape(8, 8, 128), axis=0)

    give = pltpu.make_async_copy(gv, grad_out, ls.at[0])
    give.start()

    n1[me, 0:8, :] = squares
    n1[me, 8:16, :] = jnp.broadcast_to(loss, (8, 128))
    near = [remote(n1.at[me], n1.at[me], ns.at[i], nr.at[i], p) for i, p in enumerate(dp_peers)]
    for c in near:
        c.start()
    for c in near:
        c.wait_recv()
    sums = n1[0]
    for i in range(1, 8):
        sums = sums + n1[i]
    n2[plane] = sums
    far = [remote(n2.at[plane], n2.at[plane], ms.at[i], mr.at[i], p) for i, p in enumerate(mp_peers)]
    for c in far:
        c.start()
    for c in far:
        c.wait_recv()
    sums = n2[0]
    for i in range(1, 16):
        sums = sums + n2[i]
    sums_out[...] = sums
    squared = jnp.sum(jnp.sum(sums[0:8], axis=1, keepdims=True), axis=0, keepdims=True)
    clip = jnp.minimum(1.0, MAX_NORM / (jnp.sqrt(squared) + 1e-06))

    def place(device, q):
        return pl.ds(mul_of(device * 2048 + q * 256, 256), 256)

    def block(device, q):
        return wk.at[place(device, q)]

    spread_dp = {}
    for q in range(8):
        s = 1 if q % 2 == 0 else -1
        src = {0: (me, {Z: ring(z, 1)}), 1: (me, {Z: ring(z, -1)}),
               2: (ring(z, -s) * 2 + core, {Z: ring(z, s)}),
               3: (me, {CORE: other}), 4: (ring(z, -1) * 2 + core, {CORE: other}),
               5: (ring(z, 1) * 2 + core, {CORE: other}), 6: (ring(z, 2) * 2 + core, {CORE: other})}
        for kind, (device, to) in src.items():
            b = block(device, q)
            spread_dp[q, kind] = remote(b, b, ws.at[q, kind], wr.at[q, kind], to)
    for c in state:
        c.wait()
    for q in range(8):
        rows = pl.ds(256 * q, 256)
        g = gv[rows, :] * clip
        new, _, _ = updated(g, master[rows, :], moment[rows, :], second[rows, :])
        wk[place(me, q), :] = new.astype(BF)
        for kind in (0, 1, 3):
            spread_dp[q, kind].start()
    for q in range(8):
        with_relay, against = (0, 1) if q % 2 == 0 else (1, 0)
        spread_dp[q, with_relay].wait_recv()
        spread_dp[q, 2].start()
        spread_dp[q, 4 + with_relay].start()
        spread_dp[q, against].wait_recv()
        spread_dp[q, 4 + against].start()
    out = {}

    def store(i, device):
        rows = pl.ds(mul_of(device * 2048, 2048), 2048)
        out[i] = pltpu.make_async_copy(wk.at[rows], work.at[rows], cs.at[i])
        out[i].start()

    store(0, me)
    store(1, ring(z, 1) * 2 + core)
    store(2, ring(z, -1) * 2 + core)
    for q in range(8):
        spread_dp[q, 2].wait_recv()
        spread_dp[q, 6].start()
    store(3, ring(z, 2) * 2 + core)
    for i, kind in enumerate((3, 4, 5, 6)):
        for q in range(8):
            spread_dp[q, kind].wait_recv()
        store(4 + i, ring(z, (0, -1, 1, 2)[i]) * 2 + other)
    give.wait()
    for i in out:
        out[i].wait()
    for c in swap + near + far:
        c.wait_send()
    for table in (one, two, g1, g2, hop, spread_dp):
        for key in table:
            table[key].wait_send()


def tail_kernel(grad, sums, master, moment, second, master_new, moment_new, second_new, loss):
    squared = jnp.sum(jnp.sum(sums[0:8, :], axis=1, keepdims=True), axis=0, keepdims=True)
    clip = jnp.minimum(1.0, MAX_NORM / (jnp.sqrt(squared) + 1e-06))
    new, m, v = updated(grad[...] * clip, master[...], moment[...], second[...])
    master_new[...] = new
    moment_new[...] = m
    second_new[...] = v
    loss[...] = sums[8:9, 0:1]


def updated(g, old, moment, second):
    m = 0.9 * moment + 0.1 * g
    v = 0.999 * second + 0.001 * g * g
    first_hat = m * (1.0 / (1.0 - 0.9 ** 10))
    second_hat = v * (1.0 / (1.0 - 0.999 ** 10))
    return old - 0.001 * (first_hat / (jnp.sqrt(second_hat) + 1e-08) + 0.1 * old), m, v


def rows_of(value):
    r = value.shape[0]
    return value.reshape(r, 2, 4, 128).transpose(0, 2, 1, 3).reshape(r * 8, 128)


def from_rows(value):
    r = value.shape[0] // 8
    return value.reshape(r, 4, 2, 128).transpose(0, 2, 1, 3).reshape(r, 2, 512)


def per_device(features, rewards, old_values, dones, lengths, proj_weights, down_weight, value_head,
               master, moment, second):
    dma = pltpu.SemaphoreType.DMA
    vm = pl.BlockSpec(memory_space=pltpu.VMEM)
    sm = pl.BlockSpec(memory_space=pltpu.SMEM)
    hbm = pl.BlockSpec(memory_space=pl.ANY)
    state = (rows_of(master), rows_of(moment), rows_of(second))
    rows = jax.ShapeDtypeStruct((8 * ROWS, 128), F32)
    row_scratch = pltpu.VMEM((8 * ROWS, 128), F32)
    block_scratch = pltpu.VMEM((4, ROWS, 1024), F32)
    link_scratch = pltpu.VMEM((2, 3, 16 + ROWS, 512), jnp.int16)
    work, grad, sums = pl.pallas_call(
        step_kernel,
        name="critic_step",
        out_shape=(jax.ShapeDtypeStruct((8 * D, 128), BF), rows, jax.ShapeDtypeStruct((16, 128), F32)),
        in_specs=[hbm] * 6 + [vm] * 4 + [sm],
        out_specs=(hbm, hbm, vm),
        scratch_shapes=[
            pltpu.VMEM((TOK, D), BF), pltpu.VMEM((4, D, 256), BF), pltpu.VMEM((FFL, D), BF),
            pltpu.VMEM((4, TOK, 256), F32), pltpu.VMEM((TOK, FFL), BF), pltpu.VMEM((4, TOK, 512), BF),
            pltpu.VMEM((2, 4, 3, 4, WT, 512), BF), pltpu.VMEM((2, 4, 3, WT, 512), BF), pltpu.VMEM((4, TOK, 512), BF),
            pltpu.VMEM((2, WT, D), F32), pltpu.VMEM((TOK, 2 * FFL), BF),
            row_scratch, row_scratch, row_scratch, block_scratch, block_scratch, block_scratch,
            link_scratch, link_scratch, row_scratch, pltpu.VMEM((8 * D, 128), BF),
            pltpu.VMEM((8, 16, 128), F32), pltpu.VMEM((16, 16, 128), F32),
            dma((2, 4)), dma((4,)), dma((4,)),
            dma((2, 4, 3, 4)), dma((2, 4, 3, 4)), dma((2, 4, 3)), dma((2, 4, 3)),
            dma((2, 4, 3)), dma((2, 4, 3)), dma((2, 4, 4, 3)), dma((2, 4, 4, 3)),
            dma((4,)), dma((4,)), dma((2, 3, 4)), dma((2, 3, 4)), dma((7,)), dma((7,)), dma((15,)), dma((15,)),
            dma((8, 7)), dma((8, 7)), dma((8,)), dma((1,)),
        ],
        compiler_params=pltpu.CompilerParams(collective_id=0, has_side_effects=True, vmem_limit_bytes=VMEM_LIMIT),
    )(features, rows_of(proj_weights), down_weight, *state, value_head.reshape(1, D), rewards, old_values, dones, lengths)
    block = pl.BlockSpec((512, 128), lambda i: (i, 0))
    whole = pl.BlockSpec((16, 128), lambda i: (0, 0))
    master_new, moment_new, second_new, loss = pl.pallas_call(
        tail_kernel,
        name="optimizer_state",
        grid=(4,),
        out_shape=(rows, rows, rows, jax.ShapeDtypeStruct((1, 1), F32)),
        in_specs=[block, whole, block, block, block],
        out_specs=(block, block, block, pl.BlockSpec((1, 1), lambda i: (0, 0))),
    )(grad, sums, *state)
    return (from_rows(master_new), from_rows(moment_new), from_rows(second_new), from_rows(work), loss.reshape(()))


def solution(mesh):
    finer = Mesh(mesh.devices.reshape(4, 2, 4, 4), (Z, CORE, X, Y))
    return jax.shard_map(
        per_device,
        mesh=finer,
        in_specs=(
            P(DP, None), P(DP, None), P(DP, None), P(DP, None), P(DP),
            P(None, None, MP), P(MP, None), P(),
            P(DP, None, MP), P(DP, None, MP), P(DP, None, MP),
        ),
        out_specs=(P(DP, None, MP), P(DP, None, MP), P(DP, None, MP), P(None, None, MP), P()),
        check_vma=False,
    )
```

time: 163 us -> 145 us (0.89)
  local copies, waits for them, and re-layouts: 26.3 us -> 7.7 us
  Pallas kernels: 135 us -> 137 us
    transpose x1 -> x0, local copies, waits for them, and re-layouts: 7.71 us -> none  [per_device(): proj_weights.reshape(D, 2, 4, 128).transpose(2, 0, 1, 3).reshape(4, D, 256)]
    reshape x1 -> x0, local copies, waits for them, and re-layouts: 7.59 us -> none  [per_device(): proj_weights.reshape(D, 2, 4, 128).transpose(2, 0, 1, 3).reshape(4, D, 256)]
    unnamed x6 -> x1, local copies, waits for them, and re-layouts: 9.68 us -> 7.7 us
where the time goes in v2:
time: 145 us
  Pallas kernels  137 us (94%)
  local copies, waits for them, and re-layouts  7.7 us (5%)
    pallas_call x1, Pallas kernels, per_device(): pl.pallas_call(step_kernel, name='critic_step', out_shape=(jax.ShapeDtype...  132 us
    unnamed x1, local copies, waits for them, and re-layouts  7.7 us
    pallas_call x1, Pallas kernels, per_device(): pl.pallas_call(tail_kernel, name='optimizer_state', grid=(4,), out_shape=...  4.88 us

profile of v2, /device:TPU:1, one launch (start us, length us, event | category | flops | bytes accessed | tf_op | source)
XLA Modules:
  0.0 145.1 jit_solution(15293280834695770834)
XLA Ops:
  0.6 131.9 %critic_step.1 = (bf16[16384,128]{1,0:T(8,128)(2,1)}, f32[2048,128]{1,0:T(8,128)}, f32[16,128]{1,0:T(8,128)}) custom-call(bf16[1024,2048]{1,0:T(8,128)(2,1)} %feat_hbm.1, bf16[16384,128]{1,0:T(8,128)(2,1)} %bitcast.42, bf16[512,2048]{1,0:T(8,128)(2,1)} %down_hbm.1, f32[2048,128]{1,0:T(8,128)} %bitcast.44, f32[2048,128]{1,0:T(8,128)} %bitcast.46, ...), custom_call_target="tpu_custom_call" | custom-call | tf_op jit(solution)/shard_map/critic_step/pallas_call | solution.py:577
  132.5 4.9 %optimizer_state.1 = (f32[2048,128]{1,0:T(8,128)}, f32[2048,128]{1,0:T(8,128)}, f32[2048,128]{1,0:T(8,128)}, f32[1,1]{1,0:T(1,128)}) custom-call(f32[2048,128]{1,0:T(8,128)} %get-tuple-element.12.grad, f32[16,128]{1,0:T(8,128)} %get-tuple-element.13.sums, f32[2048,128]{1,0:T(8,128)} %bitcast.45, f32[2048,128]{1,0:T(8,128)} %bitcast.47, f32[2048,128]{1,0:T(8,128)} %bitcast.49), custom_call_target="tpu_custom_call" | custom-call | tf_op jit(solution)/shard_map/optimizer_state/pallas_call | solution.py:601
  137.4 7.7 %copy.25 = bf16[2048,2,512]{2,1,0:T(2,128)(2,1)} copy(bf16[2048,2,512]{2,1,0:T(2,128)(2,1)} %bitcast.43) | data formatting | bytes 8388608

commit v3 on v2

--- a/solution.py
+++ b/solution.py
@@ -21,7 +21,7 @@
 BF = jnp.bfloat16
 LEVELS = 32000.0
 F32 = jnp.float32
-VMEM_LIMIT = 62 * 1024 * 1024
+VMEM_LIMIT = 54 * 1024 * 1024
 
 
 def mul_of(v, n):
@@ -43,7 +43,10 @@
     barrier = pltpu.get_barrier_semaphore()
     for device in devices:
         pl.semaphore_signal(barrier, inc=1, device_id=device, device_id_type=pl.DeviceIdType.MESH)
-    pl.semaphore_wait(barrier, len(devices))
+
+
+def greeted(devices):
+    pl.semaphore_wait(pltpu.get_barrier_semaphore(), len(devices))
 
 
 def own_targets(row, start, rew, old, dones, lengths):
@@ -71,12 +74,14 @@
 WAVE = 512
 
 
-def step_kernel(feat_hbm, w_hbm, down_hbm, master_hbm, moment_hbm, second_hbm, head, rew, old, dones, lengths,
-                work, grad_out, sums_out,
+def step_kernel(feat_hbm, w_hbm, down_hbm, master_hbm, moment_hbm, second_hbm,
+                head_hbm, rew_hbm, old_hbm, dones_hbm, lengths_hbm,
+                wk, mo, vo, so, sums_out,
                 feat, w4, down, both, hid, part, rv1, rv2, og, mix, bg,
-                master, moment, second, gsend, gown, grecv, qs, qr, gv, wk, n1, n2,
-                fs, rs, os, s1, r1, s2, r2, gs1, gr1, gs2, gr2,
-                ds, dr, zs, zr, ns, nr, ms, mr, ws, wr, cs, ls):
+                master, moment, second, gsend, gown, grecv, qs, qr, gv, n1, n2,
+                head, rew, old, dones, lengths,
+                ins, fs, sent, rx, ry, rfr, rtwo, rg1, rga, rgb, rgc,
+                dr, zr0, zr1, nr, wr, wd):
     z, core, x, y = (lax.axis_index(a) for a in (Z, CORE, X, Y))
     other = 1 - core
     me = z * 2 + core
@@ -84,27 +89,29 @@
     dp_peers = [{Z: ring(z, i // 2), CORE: lax.rem(core + i % 2, 2)} for i in range(1, 8)]
     mp_peers = [{X: ring(x, i // 4), Y: ring(y, i % 4)} for i in range(1, 16)]
 
+    greet(dp_peers + mp_peers)
+    loads = []
+
+    def load(src, dst):
+        loads.append(pltpu.make_async_copy(src, dst, ins.at[len(loads)]))
+        loads[-1].start()
+        return loads[-1]
+
     load_w = []
     for p in range(4):
         rows = pl.ds(4096 * p, 4096)
-        load_w.append(pltpu.make_async_copy(w_hbm.at[rows], wk.at[rows], rs.at[p]))
-        load_w[p].start()
+        load_w.append(load(w_hbm.at[rows], wk.at[rows]))
     load_f = {}
-    for w in range(2):
-        for i, dy in enumerate((2, 1, -1, 0)):
+    for i, dy in enumerate((2, 1, -1, 0)):
+        for w in range(2):
             rows = pl.ds(mul_of(ring(y, dy) * 128 + WAVE * w, 128), 128)
             load_f[w, dy] = pltpu.make_async_copy(feat_hbm.at[rows], feat.at[rows], fs.at[w, i])
-    load_d = pltpu.make_async_copy(down_hbm, down, os.at[0])
-    load_f[0, 2].start()
-    load_d.start()
-    for key in load_f:
-        if key != (0, 2):
-            load_f[key].start()
-    state = [pltpu.make_async_copy(a, b, os.at[i]) for i, a, b in
-             ((1, master_hbm, master), (2, moment_hbm, moment), (3, second_hbm, second))]
-    for c in state:
-        c.start()
-    greet(dp_peers + mp_peers)
+            load_f[w, dy].start()
+        if i == 0:
+            load_d = load(down_hbm, down)
+    small = [load(a, b) for a, b in ((head_hbm, head), (rew_hbm, rew), (old_hbm, old), (dones_hbm, dones),
+                                     (lengths_hbm, lengths))]
+    state = [load(a, b) for a, b in ((master_hbm, master), (moment_hbm, moment), (second_hbm, second))]
 
     out_row = lax.broadcasted_iota(jnp.int32, (256, 256), 0)
     in_row = lax.broadcasted_iota(jnp.int32, (256, 256), 1)
@@ -139,37 +146,58 @@
         return offsets(h).index(db)
 
     one, two, g1, g2 = {}, {}, {}, {}
+    row_at = {2: 0, 1: 1, -1: 2, 0: 3}
     for w in range(2):
         for h in range(4):
             s = STREAMS[h][1]
             for j, db in enumerate(offsets(h)):
+                relayed = rx.at[w, row_at[db]] if h < 2 else ry.at[w, h - 2]
                 for kind, (da, to) in enumerate(((2, s), (s, s), (-s, -s))):
                     one[w, h, kind, j] = remote(part.at[h, tok(w, h, da, db)], rv1.at[w, h, kind, j],
-                                                s1.at[w, h, kind, j], r1.at[w, h, kind, j], peer(True, h, to))
+                                                sent.at[0], relayed if kind == 0 else rfr.at[w, j], peer(True, h, to))
             for kind, (db, to) in enumerate(((2, s), (s, s), (-s, -s))):
                 two[w, h, kind] = remote(part.at[h, tok(w, h, 0, db)], rv2.at[w, h, kind],
-                                         s2.at[w, h, kind], r2.at[w, h, kind], peer(False, h, to))
+                                         sent.at[1], rtwo.at[w, min(kind, 1)], peer(False, h, to))
+            ahead = 0 if s == 1 else 1
             for kind, (db, to) in enumerate(((0, 1), (0, -1), (-s, s))):
                 t = og.at[h, tok(w, h, 0, db)]
-                g1[w, h, kind] = remote(t, t, gs1.at[w, h, kind], gr1.at[w, h, kind], peer(False, h, to))
+                g1[w, h, kind] = remote(t, t, sent.at[2], rg1.at[w, {ahead: 0, 1 - ahead: 1, 2: 2}[kind]],
+                                        peer(False, h, to))
             for k, db in enumerate((0, -s, s, 2)):
                 for kind, (da, to) in enumerate(((0, 1), (0, -1), (-s, s))):
                     t = og.at[h, tok(w, h, da, db)]
-                    g2[w, h, k, kind] = remote(t, t, gs2.at[w, h, k, kind], gr2.at[w, h, k, kind], peer(True, h, to))
-
-    def chunk(w, dy):
-        load_f[w, dy].wait()
-        rows = pl.ds(mul_of(ring(y, dy) * 128 + WAVE * w, 128), 128)
-        f = feat[rows, :]
+                    if kind == ahead:
+                        done = rga.at[w, k]
+                    elif h < 2:
+                        done = rgb.at[w, row_at[db]]
+                    else:
+                        done = rgc.at[w, 2 if kind == 2 else 3 - h]
+                    g2[w, h, k, kind] = remote(t, t, sent.at[3], done, peer(True, h, to))
+
+    def arrive(count, sem):
+        blocks = rv1.at[0, 0, 0, pl.ds(0, count)] if count <= 4 else rv1.at[0, pl.ds(0, count // 4), 0]
+        remote(blocks, blocks, sent.at[0], sem, {X: ring(x, 1)}).wait_recv()
+
+    def chunk(dy):
+        rows = []
+        for w in range(2):
+            load_f[w, dy].wait()
+            rows.append(pl.ds(mul_of(ring(y, dy) * 128 + WAVE * w, 128), 128))
+        f = jnp.concatenate([feat[r, :] for r in rows], axis=0)
         for c in range(4):
             gu = jnp.dot(f, w4[c], preferred_element_type=F32)
-            both[c, rows, :] = gu
             gate, up = gu[:, :128], gu[:, 128:]
-            hid[rows, c * 128:(c + 1) * 128] = (gate * jax.nn.sigmoid(gate) * up).astype(BF)
-        v = hid[rows, :]
-        for h in range(4):
-            part[h, rows, :] = jnp.dot(
-                v, down[:, h * 512:(h + 1) * 512], preferred_element_type=F32).astype(BF)
+            value = (gate * jax.nn.sigmoid(gate) * up).astype(BF)
+            hid[:, c * 128:(c + 1) * 128] = value
+            for w in range(2):
+                both[c, rows[w], :] = gu[128 * w:128 * (w + 1)]
+        v = hid[...]
+        for h in range(4):
+            product = jnp.dot(v, down[:, h * 512:(h + 1) * 512], preferred_element_type=F32).astype(BF)
+            for w in range(2):
+                part[h, rows[w], :] = product[128 * w:128 * (w + 1)]
+
+    def send(w, dy):
         for h in (0, 1):
             one[w, h, 0, index(h, dy)].start()
             one[w, h, 2, index(h, dy)].start()
@@ -183,37 +211,37 @@
                     one[w, h, 2, j].start()
 
     def pass_on(w, h, j):
-        s = STREAMS[h][1]
-        one[w, h, 0, j].wait_recv()
-        t = tok(w, h, s, offsets(h)[j])
+        t = tok(w, h, STREAMS[h][1], offsets(h)[j])
         part[h, t, :] = (part[h, t, :].astype(F32) + rv1[w, h, 0, j].astype(F32)).astype(BF)
         one[w, h, 1, j].start()
 
     def pass_x(w, dy):
+        arrive(2, rx.at[w, row_at[dy]])
         for h in (0, 1):
             pass_on(w, h, index(h, dy))
 
     def pass_y(w, h):
+        arrive(4, ry.at[w, h - 2])
         for j in range(4):
             pass_on(w, h, j)
 
     def finish_one(w, h, j):
-        one[w, h, 1, j].wait_recv()
-        one[w, h, 2, j].wait_recv()
         t = tok(w, h, 0, offsets(h)[j])
         total = part[h, t, :].astype(F32) + rv1[w, h, 1, j].astype(F32) + rv1[w, h, 2, j].astype(F32)
         if j == 3:
-            two[w, h, 1].wait_recv()
-            two[w, h, 2].wait_recv()
             mix[w, :, h * 512:(h + 1) * 512] = total + rv2[w, h, 1].astype(F32) + rv2[w, h, 2].astype(F32)
             return
         if j == 1:
-            two[w, h, 0].wait_recv()
             total = total + rv2[w, h, 0].astype(F32)
         part[h, t, :] = total.astype(BF)
         two[w, h, j].start()
 
     def finish(w, j):
+        arrive(8, rfr.at[w, j])
+        if j == 1:
+            arrive(4, rtwo.at[w, 0])
+        if j == 3:
+            arrive(8, rtwo.at[w, 1])
         for h in range(4):
             finish_one(w, h, j)
 
@@ -234,58 +262,41 @@
             og[h, mine, :] = (a * vh[:, cols] - b * stream[:, cols]).astype(BF)
         return jnp.sum(mask * errors * errors, axis=0, keepdims=True) / total_tokens
 
-    waited = set()
-
-    def arrive(name, key):
-        if (name, key) not in waited:
-            waited.add((name, key))
-            {"g1": g1, "g2": g2}[name][key].wait_recv()
-
-    def ahead(h):
-        return 0 if STREAMS[h][1] == 1 else 1
-
-    def spread(w, h, k):
-        g2[w, h, k, 0].start()
-        g2[w, h, k, 1].start()
+    def spread(w, k):
+        for h in range(4):
+            g2[w, h, k, 0].start()
+            g2[w, h, k, 1].start()
 
     def relay(w, k):
-        for h in range(4):
-            arrive("g2", (w, h, k, ahead(h)))
+        arrive(4, rga.at[w, k])
+        for h in range(4):
             g2[w, h, k, 2].start()
 
     def gather_0(w):
         for h in range(4):
             g1[w, h, 0].start()
             g1[w, h, 1].start()
-        for h in range(4):
-            spread(w, h, 0)
+        spread(w, 0)
 
     def gather_1(w):
-        for h in range(4):
-            arrive("g1", (w, h, ahead(h)))
+        arrive(4, rg1.at[w, 0])
+        for h in range(4):
             g1[w, h, 2].start()
-            spread(w, h, 1)
+        spread(w, 1)
 
     def gather_2(w):
         relay(w, 0)
-        for h in range(4):
-            arrive("g1", (w, h, 1 - ahead(h)))
-            spread(w, h, 2)
+        arrive(4, rg1.at[w, 1])
+        spread(w, 2)
 
     def gather_3(w):
-        for h in range(4):
-            arrive("g1", (w, h, 2))
-            spread(w, h, 3)
+        arrive(4, rg1.at[w, 2])
+        spread(w, 3)
 
     def backward(w, dy):
-        for h in (0, 1):
-            k = (0, -STREAMS[h][1], STREAMS[h][1], 2).index(dy)
-            for kind in range(3):
-                arrive("g2", (w, h, k, kind))
+        arrive(4, rgb.at[w, row_at[dy]])
         if dy != 0:
-            for h in (2, 3):
-                for k in range(4):
-                    arrive("g2", (w, h, k, {-1: 0, 1: 1, 2: 2}[dy]))
+            arrive({-1: 4, 1: 4, 2: 8}[dy], rgc.at[w, {-1: 0, 1: 1, 2: 2}[dy]])
         rows = pl.ds(mul_of(ring(y, dy) * 128 + WAVE * w, 128), 128)
         hg = None
         for h in range(4):
@@ -299,38 +310,45 @@
             bg[rows, c * 256:c * 256 + 128] = (d * up * sig * (1.0 + gate * (1.0 - sig))).astype(BF)
             bg[rows, c * 256 + 128:(c + 1) * 256] = (d * gate * sig).astype(BF)
 
-    chunk(0, 2)
-    chunk(0, 1)
+    chunk(2)
+    greeted(dp_peers + mp_peers)
+    send(0, 2)
+    chunk(1)
+    send(0, 1)
+    chunk(-1)
+    send(0, -1)
     pass_x(0, 2)
     pass_y(0, 2)
-    chunk(0, -1)
+    chunk(0)
+    send(0, 0)
+    send(1, 2)
     pass_x(0, 1)
     pass_y(0, 3)
-    chunk(0, 0)
     pass_x(0, -1)
-    chunk(1, 2)
+    send(1, 1)
+    for c in small:
+        c.wait()
     own = [own_targets(2 * w + y // 2, (y % 2) * 128 + x * WT, rew, old, dones, lengths) for w in range(2)]
     finish(0, 0)
+    send(1, -1)
     pass_x(0, 0)
-    chunk(1, 1)
     finish(0, 1)
+    send(1, 0)
     pass_x(1, 2)
     pass_y(1, 2)
-    chunk(1, -1)
     finish(0, 2)
-    pass_x(1, 1)
     finish(0, 3)
     loss = own_loss(0, *own[0])
+    pass_x(1, 1)
+    pass_y(1, 3)
+    pass_x(1, -1)
     gather_0(0)
-    pass_y(1, 3)
-    chunk(1, 0)
-    pass_x(1, -1)
     finish(1, 0)
     pass_x(1, 0)
+    finish(1, 1)
     gather_1(0)
-    finish(1, 1)
+    finish(1, 2)
     gather_2(0)
-    finish(1, 2)
     finish(1, 3)
     loss = loss + own_loss(1, *own[1])
     gather_0(1)
@@ -352,11 +370,13 @@
         backward(1, dy)
 
     order = (2, 1, -1, 0)
-    swap = [remote(gsend.at[i], grecv.at[i], ds.at[i], dr.at[i], {CORE: other}) for i in range(4)]
-
-    def grad_rows(dz, c):
+    halves = (slice(0, 512), slice(512, 1024))
+    swap = [[remote(gsend.at[i, :, half], grecv.at[i, :, half], sent.at[4], dr.at[i, h], {CORE: other})
+             for h, half in enumerate(halves)] for i in range(4)]
+
+    def grad_rows(dz, c, half):
         cols = pl.ds(mul_of((ring(z, dz) * 2 + c) * ROWS, ROWS), ROWS)
-        return lax.dot_general(feat[:, cols], bg[...], (((0,), (0,)), ((), ())), preferred_element_type=F32)
+        return lax.dot_general(feat[:, cols], bg[:, half], (((0,), (0,)), ((), ())), preferred_element_type=F32)
 
     hop = {}
     for h, s in enumerate((1, -1)):
@@ -364,7 +384,7 @@
             for j in range(4):
                 rows = pl.ds(0, 80) if j == 0 else pl.ds(16 + 64 * j, 64)
                 hop[h, kind, j] = remote(qs.at[h, kind, rows], qr.at[h, kind, rows],
-                                         zs.at[h, kind, j], zr.at[h, kind, j], {Z: ring(z, to)})
+                                         sent.at[5], zr0.at[h, j] if kind == 0 else zr1.at[j], {Z: ring(z, to)})
 
     def exponent_of(bound):
         return jnp.ceil(4.0 * jnp.log2(jnp.maximum(bound, 1e-30)) + 0.02)
@@ -418,28 +438,33 @@
             hop[h, 1, j].start()
 
     for i, dz in enumerate(order):
-        gsend[i] = grad_rows(dz, other)
-        swap[i].start()
-        gown[i] = grad_rows(dz, core)
+        for h, half in enumerate(halves):
+            gsend[i, :, half] = grad_rows(dz, other, half)
+            swap[i][h].start()
         if i == 1:
-            swap[0].wait_recv()
-            straight(0, 0, 0)
-            straight(0, 1, 0)
+            for h in (0, 1):
+                swap[0][h].wait_recv()
+                straight(0, h, 0)
         if i == 2:
-            swap[1].wait_recv()
+            swap[1][1].wait_recv()
             straight(1, 1, 2)
         if i == 3:
-            swap[2].wait_recv()
+            swap[2][0].wait_recv()
             straight(2, 0, 2)
+        for half in halves:
+            gown[i, :, half] = grad_rows(dz, core, half)
+    swap[1][0].wait_recv()
     pass_sum(1, 0)
+    swap[2][1].wait_recv()
     pass_sum(2, 1)
-    swap[3].wait_recv()
+    for h in (0, 1):
+        swap[3][h].wait_recv()
     squares = jnp.zeros((8, 128), F32)
     units = {}
     for j in range(4):
+        blocks = qr.at[:, pl.ds(1, 2), pl.ds(0, 80) if j == 0 else pl.ds(16 + 64 * j, 64)]
+        remote(blocks, blocks, sent.at[5], zr1.at[j], {Z: ring(z, 1)}).wait_recv()
         for h in range(2):
-            hop[h, 2, j].wait_recv()
-            hop[h, 1, j].wait_recv()
             if j == 0:
                 units[h] = [received(h, kind) / LEVELS for kind in (1, 2)]
             owned = gown[3, 64 * j:64 * (j + 1), 512 * h:512 * (h + 1)] + grecv[3, 64 * j:64 * (j + 1), 512 * h:512 * (h + 1)]
@@ -449,25 +474,21 @@
                 gv[pl.ds(64 * j * 8 + 4 * h + c, 64, stride=8), :] = piece
                 squares = squares + jnp.sum((piece * piece).reshape(8, 8, 128), axis=0)
 
-    give = pltpu.make_async_copy(gv, grad_out, ls.at[0])
-    give.start()
-
     n1[me, 0:8, :] = squares
     n1[me, 8:16, :] = jnp.broadcast_to(loss, (8, 128))
-    near = [remote(n1.at[me], n1.at[me], ns.at[i], nr.at[i], p) for i, p in enumerate(dp_peers)]
+    near = [remote(n1.at[me], n1.at[me], sent.at[6], nr.at[0], p) for p in dp_peers]
     for c in near:
         c.start()
-    for c in near:
-        c.wait_recv()
+    seven, fifteen = n1.at[pl.ds(0, 7)], n2.at[pl.ds(0, 15)]
+    remote(seven, seven, sent.at[6], nr.at[0], dp_peers[0]).wait_recv()
     sums = n1[0]
     for i in range(1, 8):
         sums = sums + n1[i]
     n2[plane] = sums
-    far = [remote(n2.at[plane], n2.at[plane], ms.at[i], mr.at[i], p) for i, p in enumerate(mp_peers)]
+    far = [remote(n2.at[plane], n2.at[plane], sent.at[7], nr.at[1], p) for p in mp_peers]
     for c in far:
         c.start()
-    for c in far:
-        c.wait_recv()
+    remote(fifteen, fifteen, sent.at[7], nr.at[1], mp_peers[0]).wait_recv()
     sums = n2[0]
     for i in range(1, 16):
         sums = sums + n2[i]
@@ -490,13 +511,16 @@
                5: (ring(z, 1) * 2 + core, {CORE: other}), 6: (ring(z, 2) * 2 + core, {CORE: other})}
         for kind, (device, to) in src.items():
             b = block(device, q)
-            spread_dp[q, kind] = remote(b, b, ws.at[q, kind], wr.at[q, kind], to)
+            spread_dp[q, kind] = remote(b, b, sent.at[8], wr.at[q, kind] if kind < 3 else wd.at[0], to)
     for c in state:
         c.wait()
     for q in range(8):
         rows = pl.ds(256 * q, 256)
         g = gv[rows, :] * clip
-        new, _, _ = updated(g, master[rows, :], moment[rows, :], second[rows, :])
+        new, m, v = updated(g, master[rows, :], moment[rows, :], second[rows, :])
+        mo[rows, :] = new
+        vo[rows, :] = m
+        so[rows, :] = v
         wk[place(me, q), :] = new.astype(BF)
         for kind in (0, 1, 3):
             spread_dp[q, kind].start()
@@ -507,42 +531,25 @@
         spread_dp[q, 4 + with_relay].start()
         spread_dp[q, against].wait_recv()
         spread_dp[q, 4 + against].start()
-    out = {}
-
-    def store(i, device):
-        rows = pl.ds(mul_of(device * 2048, 2048), 2048)
-        out[i] = pltpu.make_async_copy(wk.at[rows], work.at[rows], cs.at[i])
-        out[i].start()
-
-    store(0, me)
-    store(1, ring(z, 1) * 2 + core)
-    store(2, ring(z, -1) * 2 + core)
     for q in range(8):
         spread_dp[q, 2].wait_recv()
         spread_dp[q, 6].start()
-    store(3, ring(z, 2) * 2 + core)
-    for i, kind in enumerate((3, 4, 5, 6)):
-        for q in range(8):
-            spread_dp[q, kind].wait_recv()
-        store(4 + i, ring(z, (0, -1, 1, 2)[i]) * 2 + other)
-    give.wait()
-    for i in out:
-        out[i].wait()
-    for c in swap + near + far:
-        c.wait_send()
-    for table in (one, two, g1, g2, hop, spread_dp):
-        for key in table:
-            table[key].wait_send()
-
-
-def tail_kernel(grad, sums, master, moment, second, master_new, moment_new, second_new, loss):
-    squared = jnp.sum(jnp.sum(sums[0:8, :], axis=1, keepdims=True), axis=0, keepdims=True)
-    clip = jnp.minimum(1.0, MAX_NORM / (jnp.sqrt(squared) + 1e-06))
-    new, m, v = updated(grad[...] * clip, master[...], moment[...], second[...])
-    master_new[...] = new
-    moment_new[...] = m
-    second_new[...] = v
+    four, all_but_one = wk.at[pl.ds(0, 4 * 2048)], wk.at[pl.ds(0, 7 * 2048)]
+    remote(four, four, sent.at[8], wd.at[0], {CORE: other}).wait_recv()
+    for i, (ref, device) in enumerate(((rv1, {X: ring(x, 1)}), (rv2, {X: ring(x, 1)}), (rv2, {X: ring(x, 1)}),
+                                       (rv1, {X: ring(x, 1)}), (gsend, {CORE: other}), (qs, {Z: ring(z, 1)}),
+                                       (seven, dp_peers[0]), (fifteen, mp_peers[0]), (all_but_one, {CORE: other}))):
+        remote(ref, ref, sent.at[i], nr.at[0], device).wait_send()
+
+
+def tail_kernel(work, master, moment, second, sums, work_out, master_out, moment_out, second_out, loss, sems):
+    copies = [pltpu.make_async_copy(a, b, sems.at[i]) for i, (a, b) in enumerate((
+        (work, work_out), (master, master_out), (moment, moment_out), (second, second_out)))]
+    for c in copies:
+        c.start()
     loss[...] = sums[8:9, 0:1]
+    for c in copies:
+        c.wait()
 
 
 def updated(g, old, moment, second):
@@ -574,38 +581,39 @@
     row_scratch = pltpu.VMEM((8 * ROWS, 128), F32)
     block_scratch = pltpu.VMEM((4, ROWS, 1024), F32)
     link_scratch = pltpu.VMEM((2, 3, 16 + ROWS, 512), jnp.int16)
-    work, grad, sums = pl.pallas_call(
+    results = pl.pallas_call(
         step_kernel,
         name="critic_step",
-        out_shape=(jax.ShapeDtypeStruct((8 * D, 128), BF), rows, jax.ShapeDtypeStruct((16, 128), F32)),
-        in_specs=[hbm] * 6 + [vm] * 4 + [sm],
-        out_specs=(hbm, hbm, vm),
+        out_shape=(pltpu.VMEM((8 * D, 128), BF), row_scratch, row_scratch, row_scratch,
+                   pltpu.VMEM((16, 128), F32)),
+        in_specs=[hbm] * 11,
+        out_specs=(vm, vm, vm, vm, vm),
         scratch_shapes=[
             pltpu.VMEM((TOK, D), BF), pltpu.VMEM((4, D, 256), BF), pltpu.VMEM((FFL, D), BF),
-            pltpu.VMEM((4, TOK, 256), F32), pltpu.VMEM((TOK, FFL), BF), pltpu.VMEM((4, TOK, 512), BF),
+            pltpu.VMEM((4, TOK, 256), F32), pltpu.VMEM((256, FFL), BF), pltpu.VMEM((4, TOK, 512), BF),
             pltpu.VMEM((2, 4, 3, 4, WT, 512), BF), pltpu.VMEM((2, 4, 3, WT, 512), BF), pltpu.VMEM((4, TOK, 512), BF),
             pltpu.VMEM((2, WT, D), F32), pltpu.VMEM((TOK, 2 * FFL), BF),
             row_scratch, row_scratch, row_scratch, block_scratch, block_scratch, block_scratch,
-            link_scratch, link_scratch, row_scratch, pltpu.VMEM((8 * D, 128), BF),
+            link_scratch, link_scratch, row_scratch,
             pltpu.VMEM((8, 16, 128), F32), pltpu.VMEM((16, 16, 128), F32),
-            dma((2, 4)), dma((4,)), dma((4,)),
-            dma((2, 4, 3, 4)), dma((2, 4, 3, 4)), dma((2, 4, 3)), dma((2, 4, 3)),
-            dma((2, 4, 3)), dma((2, 4, 3)), dma((2, 4, 4, 3)), dma((2, 4, 4, 3)),
-            dma((4,)), dma((4,)), dma((2, 3, 4)), dma((2, 3, 4)), dma((7,)), dma((7,)), dma((15,)), dma((15,)),
-            dma((8, 7)), dma((8, 7)), dma((8,)), dma((1,)),
+            pltpu.VMEM((1, D), F32), pltpu.VMEM((4, 256), F32), pltpu.VMEM((4, 256), F32),
+            pltpu.VMEM((4, 256), jnp.int32), pltpu.SMEM((4,), jnp.int32),
+            dma((13,)), dma((2, 4)), dma((9,)),
+            dma((2, 4)), dma((2, 2)), dma((2, 4)), dma((2, 2)),
+            dma((2, 3)), dma((2, 4)), dma((2, 4)), dma((2, 3)),
+            dma((4, 2)), dma((2, 4)), dma((4,)), dma((2,)), dma((8, 3)), dma((1,)),
         ],
         compiler_params=pltpu.CompilerParams(collective_id=0, has_side_effects=True, vmem_limit_bytes=VMEM_LIMIT),
     )(features, rows_of(proj_weights), down_weight, *state, value_head.reshape(1, D), rewards, old_values, dones, lengths)
-    block = pl.BlockSpec((512, 128), lambda i: (i, 0))
-    whole = pl.BlockSpec((16, 128), lambda i: (0, 0))
-    master_new, moment_new, second_new, loss = pl.pallas_call(
+    work, master_new, moment_new, second_new, loss = pl.pallas_call(
         tail_kernel,
-        name="optimizer_state",
-        grid=(4,),
-        out_shape=(rows, rows, rows, jax.ShapeDtypeStruct((1, 1), F32)),
-        in_specs=[block, whole, block, block, block],
-        out_specs=(block, block, block, pl.BlockSpec((1, 1), lambda i: (0, 0))),
-    )(grad, sums, *state)
+        name="results",
+        out_shape=(jax.ShapeDtypeStruct((8 * D, 128), BF), rows, rows, rows, jax.ShapeDtypeStruct((1, 1), F32)),
+        in_specs=[vm] * 5,
+        out_specs=(hbm, hbm, hbm, hbm, vm),
+        scratch_shapes=[dma((4,))],
+        compiler_params=pltpu.CompilerParams(vmem_limit_bytes=4 * 1024 * 1024),
+    )(*(pltpu.with_memory_space_constraint(r, pltpu.VMEM) for r in results))
     return (from_rows(master_new), from_rows(moment_new), from_rows(second_new), from_rows(work), loss.reshape(()))
 
 

time: 145 us -> 124 us (0.86)
  Pallas kernels: 137 us -> 123 us
  local copies, waits for them, and re-layouts: 7.7 us -> 0 us
    pallas_call x2, Pallas kernels: 137 us -> 123 us  [the longest x1 119 us: per_device(): pl.pallas_call(step_kernel, name='critic_step', out_shape=(pltpu.VMEM((8...]
    unnamed x1 -> x0, local copies, waits for them, and re-layouts: 7.7 us -> none
where the time goes in v3:
time: 124 us; the launch traced here: 123 us
  Pallas kernels  123 us (99%)
    pallas_call x1, Pallas kernels, per_device(): pl.pallas_call(step_kernel, name='critic_step', out_shape=(pltpu.VMEM((8...  119 us
    pallas_call x1, Pallas kernels, per_device(): pl.pallas_call(tail_kernel, name='results', out_shape=(jax.ShapeDtypeStru...  3.53 us

profile of v3, /device:TPU:1, one launch (start us, length us, event | category | flops | bytes accessed | tf_op | source)
XLA Modules:
  0.0 123.4 jit_solution(13427635321159839960)
XLA Ops:
  0.6 119.1 %critic_step.1 = (bf16[16384,128]{1,0:T(8,128)(2,1)S(1)}, f32[2048,128]{1,0:T(8,128)S(1)}, f32[2048,128]{1,0:T(8,128)S(1)}, f32[2048,128]{1,0:T(8,128)S(1)}, f32[16,128]{1,0:T(8,128)S(1)}) custom-call(bf16[1024,2048]{1,0:T(8,128)(2,1)} %feat_hbm.1, bf16[16384,128]{1,0:T(8,128)(2,1)} %bitcast.42, bf16[512,2048]{1,0:T(8,128)(2,1)} %down_hbm.1, ...), custom_call_target="tpu_custom_call" | custom-call | tf_op jit(solution)/shard_map/critic_step/pallas_call | solution.py:584
  119.7 3.5 %results.1 = (bf16[16384,128]{1,0:T(8,128)(2,1)}, f32[2048,128]{1,0:T(8,128)}, f32[2048,128]{1,0:T(8,128)}, f32[2048,128]{1,0:T(8,128)}, f32[1,1]{1,0:T(1,128)}) custom-call(bf16[16384,128]{1,0:T(8,128)(2,1)S(1)} %get-tuple-element.15.work, f32[2048,128]{1,0:T(8,128)S(1)} %get-tuple-element.16.master, f32[2048,128]{1,0:T(8,128)S(1)} %get-tuple-element.17.moment, ...), custom_call_target="tpu_custom_call" | custom-call | tf_op jit(solution)/shard_map/results/pallas_call | solution.py:608

commit v4 on v3

--- a/solution.py
+++ b/solution.py
@@ -72,6 +72,22 @@
 STREAMS = ((True, 1), (True, -1), (False, 1), (False, -1))
 WT = 32
 WAVE = 512
+ORDER = (
+    ("C", 2), ("S", 0, 2, 1), ("S", 0, 2, 0), ("S", 1, 2, 1), ("C", 1), ("S", 0, 1, 0), ("C", -1),
+    ("S", 0, -1, 0), ("C", 0), ("PX", 0, 2), ("S", 0, 0, 0), ("S", 1, 2, 0), ("S", 1, 1, 1), ("S", 1, -1, 1),
+    ("S", 1, -1, 0), ("S", 1, 1, 0), ("PX", 0, 1), ("S", 0, -1, 1), ("S", 0, 1, 1), ("S", 1, 0, 0),
+    ("PY", 0, 2), ("PY", 0, 3), ("PX", 0, -1), ("FN", 0, 0, 0), ("PY", 1, 2), ("PX", 0, 0), ("PY", 1, 3),
+    ("PX", 1, 2), ("PX", 1, -1), ("PX", 1, 1), ("FN", 0, 0, 1), ("PX", 1, 0), ("FN", 0, 2, 1),
+    ("FN", 0, 2, 0), ("FN", 0, 1, 0), ("FN", 1, 0, 0), ("FN", 1, 0, 1), ("FN", 1, 2, 0), ("FN", 1, 2, 1),
+    ("FN", 0, 1, 1), ("FN", 0, 3, 0), ("FN", 1, 1, 1), ("FN", 1, 1, 0), ("FN", 0, 3, 1), ("L", 0),
+    ("G0", 0, 1), ("G0", 0, 0), ("G0b", 0, 0), ("G0b", 0, 1), ("FN", 1, 3, 1), ("FN", 1, 3, 0), ("L", 1),
+    ("G0", 1, 0), ("G0", 1, 1), ("G0b", 1, 0), ("G0b", 1, 1), ("G2", 0, 1), ("G1", 0, 1), ("G1", 0, 0),
+    ("G2", 0, 0), ("R", 0, 0, 0), ("R", 0, 0, 1), ("G2", 1, 1), ("G2", 1, 0), ("G1", 1, 0), ("G1", 1, 1),
+    ("R", 1, 0, 0), ("R", 1, 0, 1), ("G3", 0, 1), ("R", 0, 2, 1), ("R", 0, 1, 0), ("R", 0, 1, 1),
+    ("R", 0, 2, 0), ("G3", 0, 0), ("B", 0, 0), ("R", 1, 2, 0), ("R", 1, 2, 1), ("G3", 1, 0), ("R", 1, 1, 0),
+    ("G3", 1, 1), ("R", 1, 1, 1), ("B", 1, 0), ("R", 0, 3, 1), ("B", 0, 1), ("B", 0, -1), ("R", 0, 3, 0),
+    ("R", 1, 3, 0), ("R", 1, 3, 1), ("B", 1, -1), ("B", 1, 1), ("B", 0, 2), ("B", 1, 2),
+)
 
 
 def step_kernel(feat_hbm, w_hbm, down_hbm, master_hbm, moment_hbm, second_hbm,
@@ -106,18 +122,20 @@
         for w in range(2):
             rows = pl.ds(mul_of(ring(y, dy) * 128 + WAVE * w, 128), 128)
             load_f[w, dy] = pltpu.make_async_copy(feat_hbm.at[rows], feat.at[rows], fs.at[w, i])
-            load_f[w, dy].start()
-        if i == 0:
-            load_d = load(down_hbm, down)
-    small = [load(a, b) for a, b in ((head_hbm, head), (rew_hbm, rew), (old_hbm, old), (dones_hbm, dones),
-                                     (lengths_hbm, lengths))]
-    state = [load(a, b) for a, b in ((master_hbm, master), (moment_hbm, moment), (second_hbm, second))]
+    load_f[0, 2].start()
+    load_f[1, 2].start()
+    load_d = load(down_hbm, down)
+    small, state = [], []
 
     out_row = lax.broadcasted_iota(jnp.int32, (256, 256), 0)
     in_row = lax.broadcasted_iota(jnp.int32, (256, 256), 1)
     select = jnp.where(in_row == (out_row % 32) * 8 + out_row // 32, 1.0, 0.0).astype(BF)
     for p in range(4):
         load_w[p].wait()
+        if p == 2:
+            for dy in (1, -1, 0):
+                load_f[0, dy].start()
+                load_f[1, dy].start()
         for u in range(8):
             base = 4096 * p + 512 * u
             pair = jnp.concatenate([wk[base:base + 256, :], wk[base + 256:base + 512, :]], axis=1)
@@ -154,20 +172,21 @@
                 relayed = rx.at[w, row_at[db]] if h < 2 else ry.at[w, h - 2]
                 for kind, (da, to) in enumerate(((2, s), (s, s), (-s, -s))):
                     one[w, h, kind, j] = remote(part.at[h, tok(w, h, da, db)], rv1.at[w, h, kind, j],
-                                                sent.at[0], relayed if kind == 0 else rfr.at[w, j], peer(True, h, to))
+                                                sent.at[0], relayed if kind == 0 else rfr.at[w, j, h // 2],
+                                                peer(True, h, to))
             for kind, (db, to) in enumerate(((2, s), (s, s), (-s, -s))):
                 two[w, h, kind] = remote(part.at[h, tok(w, h, 0, db)], rv2.at[w, h, kind],
-                                         sent.at[1], rtwo.at[w, min(kind, 1)], peer(False, h, to))
+                                         sent.at[1], rtwo.at[w, min(kind, 1), h // 2], peer(False, h, to))
             ahead = 0 if s == 1 else 1
             for kind, (db, to) in enumerate(((0, 1), (0, -1), (-s, s))):
                 t = og.at[h, tok(w, h, 0, db)]
-                g1[w, h, kind] = remote(t, t, sent.at[2], rg1.at[w, {ahead: 0, 1 - ahead: 1, 2: 2}[kind]],
+                g1[w, h, kind] = remote(t, t, sent.at[2], rg1.at[w, {ahead: 0, 1 - ahead: 1, 2: 2}[kind], h // 2],
                                         peer(False, h, to))
             for k, db in enumerate((0, -s, s, 2)):
                 for kind, (da, to) in enumerate(((0, 1), (0, -1), (-s, s))):
                     t = og.at[h, tok(w, h, da, db)]
                     if kind == ahead:
-                        done = rga.at[w, k]
+                        done = rga.at[w, k, h // 2]
                     elif h < 2:
                         done = rgb.at[w, row_at[db]]
                     else:
@@ -197,17 +216,17 @@
             for w in range(2):
                 part[h, rows[w], :] = product[128 * w:128 * (w + 1)]
 
-    def send(w, dy):
-        for h in (0, 1):
-            one[w, h, 0, index(h, dy)].start()
-            one[w, h, 2, index(h, dy)].start()
-        for h in (2, 3):
-            s = STREAMS[h][1]
-            if dy == 2:
-                for j in range(4):
+    def send(w, dy, q):
+        if q == 0:
+            for kind in (0, 2):
+                for h in (0, 1):
+                    one[w, h, kind, index(h, dy)].start()
+            return
+        for j in range(4):
+            for h in (2, 3):
+                if dy == 2:
                     one[w, h, 0, j].start()
-            elif dy == -s:
-                for j in range(4):
+                elif dy == -STREAMS[h][1]:
                     one[w, h, 2, j].start()
 
     def pass_on(w, h, j):
@@ -236,13 +255,13 @@
         part[h, t, :] = total.astype(BF)
         two[w, h, j].start()
 
-    def finish(w, j):
-        arrive(8, rfr.at[w, j])
+    def finish(w, j, q):
+        arrive(4, rfr.at[w, j, q])
         if j == 1:
-            arrive(4, rtwo.at[w, 0])
+            arrive(2, rtwo.at[w, 0, q])
         if j == 3:
-            arrive(8, rtwo.at[w, 1])
-        for h in range(4):
+            arrive(4, rtwo.at[w, 1, q])
+        for h in (2 * q, 2 * q + 1):
             finish_one(w, h, j)
 
     def own_loss(w, targets, mask):
@@ -262,36 +281,34 @@
             og[h, mine, :] = (a * vh[:, cols] - b * stream[:, cols]).astype(BF)
         return jnp.sum(mask * errors * errors, axis=0, keepdims=True) / total_tokens
 
-    def spread(w, k):
-        for h in range(4):
-            g2[w, h, k, 0].start()
-            g2[w, h, k, 1].start()
-
-    def relay(w, k):
-        arrive(4, rga.at[w, k])
-        for h in range(4):
+    def spread(w, k, q):
+        for kind in (0, 1):
+            for h in (2 * q, 2 * q + 1):
+                g2[w, h, k, kind].start()
+
+    def relay(w, k, q):
+        arrive(2, rga.at[w, k, q])
+        for h in (2 * q, 2 * q + 1):
             g2[w, h, k, 2].start()
 
-    def gather_0(w):
-        for h in range(4):
-            g1[w, h, 0].start()
-            g1[w, h, 1].start()
-        spread(w, 0)
-
-    def gather_1(w):
-        arrive(4, rg1.at[w, 0])
-        for h in range(4):
+    def gather_0(w, q):
+        for kind in (0, 1):
+            for h in (2 * q, 2 * q + 1):
+                g1[w, h, kind].start()
+
+    def gather_1(w, q):
+        arrive(2, rg1.at[w, 0, q])
+        for h in (2 * q, 2 * q + 1):
             g1[w, h, 2].start()
-        spread(w, 1)
-
-    def gather_2(w):
-        relay(w, 0)
-        arrive(4, rg1.at[w, 1])
-        spread(w, 2)
-
-    def gather_3(w):
-        arrive(4, rg1.at[w, 2])
-        spread(w, 3)
+        spread(w, 1, q)
+
+    def gather_2(w, q):
+        arrive(2, rg1.at[w, 1, q])
+        spread(w, 2, q)
+
+    def gather_3(w, q):
+        arrive(2, rg1.at[w, 2, q])
+        spread(w, 3, q)
 
     def backward(w, dy):
         arrive(4, rgb.at[w, row_at[dy]])
@@ -310,64 +327,25 @@
             bg[rows, c * 256:c * 256 + 128] = (d * up * sig * (1.0 + gate * (1.0 - sig))).astype(BF)
             bg[rows, c * 256 + 128:(c + 1) * 256] = (d * gate * sig).astype(BF)
 
-    chunk(2)
-    greeted(dp_peers + mp_peers)
-    send(0, 2)
-    chunk(1)
-    send(0, 1)
-    chunk(-1)
-    send(0, -1)
-    pass_x(0, 2)
-    pass_y(0, 2)
-    chunk(0)
-    send(0, 0)
-    send(1, 2)
-    pass_x(0, 1)
-    pass_y(0, 3)
-    pass_x(0, -1)
-    send(1, 1)
-    for c in small:
-        c.wait()
-    own = [own_targets(2 * w + y // 2, (y % 2) * 128 + x * WT, rew, old, dones, lengths) for w in range(2)]
-    finish(0, 0)
-    send(1, -1)
-    pass_x(0, 0)
-    finish(0, 1)
-    send(1, 0)
-    pass_x(1, 2)
-    pass_y(1, 2)
-    finish(0, 2)
-    finish(0, 3)
-    loss = own_loss(0, *own[0])
-    pass_x(1, 1)
-    pass_y(1, 3)
-    pass_x(1, -1)
-    gather_0(0)
-    finish(1, 0)
-    pass_x(1, 0)
-    finish(1, 1)
-    gather_1(0)
-    finish(1, 2)
-    gather_2(0)
-    finish(1, 3)
-    loss = loss + own_loss(1, *own[1])
-    gather_0(1)
-    gather_3(0)
-    relay(0, 1)
-    gather_1(1)
-    relay(0, 2)
-    relay(0, 3)
-    gather_2(1)
-    backward(0, 0)
-    gather_3(1)
-    backward(0, -1)
-    relay(1, 1)
-    backward(0, 1)
-    relay(1, 2)
-    backward(0, 2)
-    relay(1, 3)
-    for dy in (0, -1, 1, 2):
-        backward(1, dy)
+    own, losses = [], []
+
+    def loss_of(w):
+        losses.append(own_loss(w, *own[w]))
+
+    steps = {"C": chunk, "S": send, "PX": pass_x, "PY": pass_y, "FN": finish, "L": loss_of, "G0": gather_0,
+             "G0b": lambda w, q: spread(w, 0, q), "G1": gather_1, "G2": gather_2, "G3": gather_3, "R": relay, "B": backward}
+    for at, (name, *args) in enumerate(ORDER):
+        if name == "FN" and not own:
+            for c in small:
+                c.wait()
+            own.extend(own_targets(2 * w + y // 2, (y % 2) * 128 + x * WT, rew, old, dones, lengths) for w in range(2))
+        steps[name](*args)
+        if at == 0:
+            greeted(dp_peers + mp_peers)
+            small.extend(load(a, b) for a, b in ((head_hbm, head), (rew_hbm, rew), (old_hbm, old), (dones_hbm, dones),
+                                                 (lengths_hbm, lengths)))
+            state.extend(load(a, b) for a, b in ((master_hbm, master), (moment_hbm, moment), (second_hbm, second)))
+    loss = losses[0] + losses[1]
 
     order = (2, 1, -1, 0)
     halves = (slice(0, 512), slice(512, 1024))
@@ -474,8 +452,8 @@
                 gv[pl.ds(64 * j * 8 + 4 * h + c, 64, stride=8), :] = piece
                 squares = squares + jnp.sum((piece * piece).reshape(8, 8, 128), axis=0)
 
-    n1[me, 0:8, :] = squares
-    n1[me, 8:16, :] = jnp.broadcast_to(loss, (8, 128))
+    line = lax.broadcasted_iota(jnp.int32, (8, 128), 0)
+    n1[me] = jnp.where(line == 0, jnp.sum(squares, axis=0, keepdims=True), jnp.where(line == 1, loss, 0.0))
     near = [remote(n1.at[me], n1.at[me], sent.at[6], nr.at[0], p) for p in dp_peers]
     for c in near:
         c.start()
@@ -493,7 +471,7 @@
     for i in range(1, 16):
         sums = sums + n2[i]
     sums_out[...] = sums
-    squared = jnp.sum(jnp.sum(sums[0:8], axis=1, keepdims=True), axis=0, keepdims=True)
+    squared = jnp.sum(sums[0:1], axis=1, keepdims=True)
     clip = jnp.minimum(1.0, MAX_NORM / (jnp.sqrt(squared) + 1e-06))
 
     def place(device, q):
@@ -543,11 +521,12 @@
 
 
 def tail_kernel(work, master, moment, second, sums, work_out, master_out, moment_out, second_out, loss, sems):
-    copies = [pltpu.make_async_copy(a, b, sems.at[i]) for i, (a, b) in enumerate((
-        (work, work_out), (master, master_out), (moment, moment_out), (second, second_out)))]
+    pieces = [(work.at[pl.ds(2048 * i, 2048)], work_out.at[pl.ds(2048 * i, 2048)]) for i in range(8)]
+    pieces += [(master, master_out), (moment, moment_out), (second, second_out)]
+    copies = [pltpu.make_async_copy(a, b, sems.at[i]) for i, (a, b) in enumerate(pieces)]
     for c in copies:
         c.start()
-    loss[...] = sums[8:9, 0:1]
+    loss[...] = sums[1:2, 0:1]
     for c in copies:
         c.wait()
 
@@ -585,7 +564,7 @@
         step_kernel,
         name="critic_step",
         out_shape=(pltpu.VMEM((8 * D, 128), BF), row_scratch, row_scratch, row_scratch,
-                   pltpu.VMEM((16, 128), F32)),
+                   pltpu.VMEM((8, 128), F32)),
         in_specs=[hbm] * 11,
         out_specs=(vm, vm, vm, vm, vm),
         scratch_shapes=[
@@ -595,12 +574,12 @@
             pltpu.VMEM((2, WT, D), F32), pltpu.VMEM((TOK, 2 * FFL), BF),
             row_scratch, row_scratch, row_scratch, block_scratch, block_scratch, block_scratch,
             link_scratch, link_scratch, row_scratch,
-            pltpu.VMEM((8, 16, 128), F32), pltpu.VMEM((16, 16, 128), F32),
+            pltpu.VMEM((8, 8, 128), F32), pltpu.VMEM((16, 8, 128), F32),
             pltpu.VMEM((1, D), F32), pltpu.VMEM((4, 256), F32), pltpu.VMEM((4, 256), F32),
             pltpu.VMEM((4, 256), jnp.int32), pltpu.SMEM((4,), jnp.int32),
             dma((13,)), dma((2, 4)), dma((9,)),
-            dma((2, 4)), dma((2, 2)), dma((2, 4)), dma((2, 2)),
-            dma((2, 3)), dma((2, 4)), dma((2, 4)), dma((2, 3)),
+            dma((2, 4)), dma((2, 2)), dma((2, 4, 2)), dma((2, 2, 2)),
+            dma((2, 3, 2)), dma((2, 4, 2)), dma((2, 4)), dma((2, 3)),
             dma((4, 2)), dma((2, 4)), dma((4,)), dma((2,)), dma((8, 3)), dma((1,)),
         ],
         compiler_params=pltpu.CompilerParams(collective_id=0, has_side_effects=True, vmem_limit_bytes=VMEM_LIMIT),
@@ -611,7 +590,7 @@
         out_shape=(jax.ShapeDtypeStruct((8 * D, 128), BF), rows, rows, rows, jax.ShapeDtypeStruct((1, 1), F32)),
         in_specs=[vm] * 5,
         out_specs=(hbm, hbm, hbm, hbm, vm),
-        scratch_shapes=[dma((4,))],
+        scratch_shapes=[dma((11,))],
         compiler_params=pltpu.CompilerParams(vmem_limit_bytes=4 * 1024 * 1024),
     )(*(pltpu.with_memory_space_constraint(r, pltpu.VMEM) for r in results))
     return (from_rows(master_new), from_rows(moment_new), from_rows(second_new), from_rows(work), loss.reshape(()))

time: 124 us -> 119 us (0.960)
  Pallas kernels: 123 us -> 118 us
    pallas_call x1, Pallas kernels: 119 us -> 115 us  [per_device(): pl.pallas_call(step_kernel, name='critic_step', out_shape=(pltpu.VMEM((8...]
where the time goes in v4:
time: 119 us
  Pallas kernels  118 us (99%)
    pallas_call x1, Pallas kernels, per_device(): pl.pallas_call(step_kernel, name='critic_step', out_shape=(pltpu.VMEM((8...  115 us
    pallas_call x1, Pallas kernels, per_device(): pl.pallas_call(tail_kernel, name='results', out_shape=(jax.ShapeDtypeStru...  3.59 us

profile of v4, /device:TPU:1, one launch (start us, length us, event | category | flops | bytes accessed | tf_op | source)
XLA Modules:
  0.0 119.2 jit_solution(14401894230056384419)
XLA Ops:
  0.6 114.8 %critic_step.1 = (bf16[16384,128]{1,0:T(8,128)(2,1)S(1)}, f32[2048,128]{1,0:T(8,128)S(1)}, f32[2048,128]{1,0:T(8,128)S(1)}, f32[2048,128]{1,0:T(8,128)S(1)}, f32[8,128]{1,0:T(8,128)S(1)}) custom-call(bf16[1024,2048]{1,0:T(8,128)(2,1)} %feat_hbm.1, bf16[16384,128]{1,0:T(8,128)(2,1)} %bitcast.42, bf16[512,2048]{1,0:T(8,128)(2,1)} %down_hbm.1, ...), custom_call_target="tpu_custom_call" | custom-call | tf_op jit(solution)/shard_map/critic_step/pallas_call | solution.py:563
  115.4 3.6 %results.1 = (bf16[16384,128]{1,0:T(8,128)(2,1)}, f32[2048,128]{1,0:T(8,128)}, f32[2048,128]{1,0:T(8,128)}, f32[2048,128]{1,0:T(8,128)}, f32[1,1]{1,0:T(1,128)}) custom-call(bf16[16384,128]{1,0:T(8,128)(2,1)S(1)} %get-tuple-element.15.work, f32[2048,128]{1,0:T(8,128)S(1)} %get-tuple-element.16.master, f32[2048,128]{1,0:T(8,128)S(1)} %get-tuple-element.17.moment, ...), custom_call_target="tpu_custom_call" | custom-call | tf_op jit(solution)/shard_map/results/pallas_call | solution.py:587

commit v5 on v4

--- a/solution.py
+++ b/solution.py
@@ -73,20 +73,20 @@
 WT = 32
 WAVE = 512
 ORDER = (
-    ("C", 2), ("S", 0, 2, 1), ("S", 0, 2, 0), ("S", 1, 2, 1), ("C", 1), ("S", 0, 1, 0), ("C", -1),
-    ("S", 0, -1, 0), ("C", 0), ("PX", 0, 2), ("S", 0, 0, 0), ("S", 1, 2, 0), ("S", 1, 1, 1), ("S", 1, -1, 1),
-    ("S", 1, -1, 0), ("S", 1, 1, 0), ("PX", 0, 1), ("S", 0, -1, 1), ("S", 0, 1, 1), ("S", 1, 0, 0),
-    ("PY", 0, 2), ("PY", 0, 3), ("PX", 0, -1), ("FN", 0, 0, 0), ("PY", 1, 2), ("PX", 0, 0), ("PY", 1, 3),
-    ("PX", 1, 2), ("PX", 1, -1), ("PX", 1, 1), ("FN", 0, 0, 1), ("PX", 1, 0), ("FN", 0, 2, 1),
-    ("FN", 0, 2, 0), ("FN", 0, 1, 0), ("FN", 1, 0, 0), ("FN", 1, 0, 1), ("FN", 1, 2, 0), ("FN", 1, 2, 1),
-    ("FN", 0, 1, 1), ("FN", 0, 3, 0), ("FN", 1, 1, 1), ("FN", 1, 1, 0), ("FN", 0, 3, 1), ("L", 0),
-    ("G0", 0, 1), ("G0", 0, 0), ("G0b", 0, 0), ("G0b", 0, 1), ("FN", 1, 3, 1), ("FN", 1, 3, 0), ("L", 1),
-    ("G0", 1, 0), ("G0", 1, 1), ("G0b", 1, 0), ("G0b", 1, 1), ("G2", 0, 1), ("G1", 0, 1), ("G1", 0, 0),
-    ("G2", 0, 0), ("R", 0, 0, 0), ("R", 0, 0, 1), ("G2", 1, 1), ("G2", 1, 0), ("G1", 1, 0), ("G1", 1, 1),
-    ("R", 1, 0, 0), ("R", 1, 0, 1), ("G3", 0, 1), ("R", 0, 2, 1), ("R", 0, 1, 0), ("R", 0, 1, 1),
-    ("R", 0, 2, 0), ("G3", 0, 0), ("B", 0, 0), ("R", 1, 2, 0), ("R", 1, 2, 1), ("G3", 1, 0), ("R", 1, 1, 0),
-    ("G3", 1, 1), ("R", 1, 1, 1), ("B", 1, 0), ("R", 0, 3, 1), ("B", 0, 1), ("B", 0, -1), ("R", 0, 3, 0),
-    ("R", 1, 3, 0), ("R", 1, 3, 1), ("B", 1, -1), ("B", 1, 1), ("B", 0, 2), ("B", 1, 2),
+    ("C", 2), ("S", 0, 2, 1), ("S", 0, 2, 0), ("C", 1), ("S", 1, 2, 1), ("S", 1, 1, 0), ("S", 0, 1, 1),
+    ("S", 1, 2, 0), ("S", 0, 1, 0), ("C", -1), ("S", 0, -1, 1), ("S", 0, -1, 0), ("C", 0), ("PX", 0, 2),
+    ("S", 0, 0, 0), ("PX", 1, 1), ("PY", 0, 2), ("PY", 0, 3), ("PX", 1, 2), ("PX", 0, 1), ("PY", 1, 2),
+    ("PY", 1, 3), ("PX", 0, -1), ("S", 1, -1, 0), ("FN", 0, 0, 0), ("PX", 0, 0), ("FN", 0, 0, 1),
+    ("S", 1, 1, 1), ("S", 1, -1, 1), ("S", 1, 0, 0), ("FN", 0, 2, 1), ("FN", 1, 0, 0), ("FN", 0, 2, 0),
+    ("PX", 1, -1), ("FN", 0, 1, 0), ("FN", 0, 1, 1), ("FN", 1, 0, 1), ("PX", 1, 0), ("FN", 1, 2, 1),
+    ("FN", 1, 2, 0), ("FN", 1, 1, 0), ("FN", 0, 3, 1), ("FN", 1, 1, 1), ("FN", 0, 3, 0), ("L", 0),
+    ("G0", 0, 0), ("G0", 0, 1), ("G0b", 0, 1), ("G0b", 0, 0), ("FN", 1, 3, 0), ("FN", 1, 3, 1), ("L", 1),
+    ("G0b", 1, 1), ("G0b", 1, 0), ("G0", 1, 0), ("G0", 1, 1), ("G2", 0, 0), ("G1", 0, 0), ("G1", 0, 1),
+    ("G2", 0, 1), ("T", 0), ("R", 0, 0, 1), ("R", 0, 0, 0), ("R", 1, 0, 1), ("R", 1, 0, 0), ("G2", 1, 0),
+    ("G2", 1, 1), ("G1", 1, 1), ("G1", 1, 0), ("G3", 0, 0), ("R", 0, 2, 0), ("R", 0, 1, 1), ("R", 0, 1, 0),
+    ("R", 0, 2, 1), ("G3", 0, 1), ("B", 0, 0), ("T", 1), ("R", 1, 2, 1), ("R", 1, 2, 0), ("G3", 1, 1),
+    ("R", 1, 1, 1), ("G3", 1, 0), ("B", 1, 0), ("R", 1, 1, 0), ("R", 0, 3, 0), ("R", 0, 3, 1), ("B", 0, -1),
+    ("B", 0, 1), ("R", 1, 3, 1), ("R", 1, 3, 0), ("B", 1, -1), ("B", 1, 1), ("B", 0, 2), ("B", 1, 2),
 )
 
 
@@ -329,11 +329,17 @@
 
     own, losses = [], []
 
+    def first_columns(c):
+        cols = pl.ds(mul_of((ring(z, 2) * 2 + (other if c == 0 else core)) * ROWS, ROWS), ROWS)
+        for m in range(4):
+            w4[c, 256 * m:256 * (m + 1), :] = feat[256 * m:256 * (m + 1), cols].T
+
     def loss_of(w):
         losses.append(own_loss(w, *own[w]))
 
     steps = {"C": chunk, "S": send, "PX": pass_x, "PY": pass_y, "FN": finish, "L": loss_of, "G0": gather_0,
-             "G0b": lambda w, q: spread(w, 0, q), "G1": gather_1, "G2": gather_2, "G3": gather_3, "R": relay, "B": backward}
+             "G0b": lambda w, q: spread(w, 0, q), "G1": gather_1, "G2": gather_2, "G3": gather_3, "R": relay, "B": backward,
+             "T": first_columns}
     for at, (name, *args) in enumerate(ORDER):
         if name == "FN" and not own:
             for c in small:
@@ -415,7 +421,22 @@
             qs[h, 1, 16 + 64 * j:80 + 64 * j, :] = code(mine_of(i, h, j) + value_of(h, 0, j, far_size / LEVELS), scale)
             hop[h, 1, j].start()
 
+    def first_rows(c, cols):
+        total = None
+        for m in range(4):
+            term = jnp.dot(w4[c, 256 * m:256 * (m + 1), :], bg[256 * m:256 * (m + 1), cols], preferred_element_type=F32)
+            total = term if total is None else total + term
+        return total
+
+    for q in range(4):
+        quarter = slice(256 * q, 256 * (q + 1))
+        gsend[0, :, quarter] = first_rows(0, quarter)
+        remote(gsend.at[0, :, quarter], grecv.at[0, :, quarter], sent.at[4], dr.at[0, q // 2], {CORE: other}).start()
+    for half in halves:
+        gown[0, :, half] = first_rows(1, half)
     for i, dz in enumerate(order):
+        if i == 0:
+            continue
         for h, half in enumerate(halves):
             gsend[i, :, half] = grad_rows(dz, other, half)
             swap[i][h].start()

time: 119 us -> 118 us (level)
    pallas_call x1, Pallas kernels: 115 us -> 113 us  [per_device(): pl.pallas_call(step_kernel, name='critic_step', out_shape=(pltpu.VMEM((8...]
where the time goes in v5:
time: 118 us
  Pallas kernels  117 us (99%)
    pallas_call x1, Pallas kernels, per_device(): pl.pallas_call(step_kernel, name='critic_step', out_shape=(pltpu.VMEM((8...  113 us
    pallas_call x1, Pallas kernels, per_device(): pl.pallas_call(tail_kernel, name='results', out_shape=(jax.ShapeDtypeStru...  3.59 us

profile of v5, /device:TPU:1, one launch (start us, length us, event | category | flops | bytes accessed | tf_op | source)
XLA Modules:
  0.0 117.5 jit_solution(11578904381551472449)
XLA Ops:
  0.6 113.1 %critic_step.1 = (bf16[16384,128]{1,0:T(8,128)(2,1)S(1)}, f32[2048,128]{1,0:T(8,128)S(1)}, f32[2048,128]{1,0:T(8,128)S(1)}, f32[2048,128]{1,0:T(8,128)S(1)}, f32[8,128]{1,0:T(8,128)S(1)}) custom-call(bf16[1024,2048]{1,0:T(8,128)(2,1)} %feat_hbm.1, bf16[16384,128]{1,0:T(8,128)(2,1)} %bitcast.42, bf16[512,2048]{1,0:T(8,128)(2,1)} %down_hbm.1, ...), custom_call_target="tpu_custom_call" | custom-call | tf_op jit(solution)/shard_map/critic_step/pallas_call | solution.py:584
  113.8 3.6 %results.1 = (bf16[16384,128]{1,0:T(8,128)(2,1)}, f32[2048,128]{1,0:T(8,128)}, f32[2048,128]{1,0:T(8,128)}, f32[2048,128]{1,0:T(8,128)}, f32[1,1]{1,0:T(1,128)}) custom-call(bf16[16384,128]{1,0:T(8,128)(2,1)S(1)} %get-tuple-element.15.work, f32[2048,128]{1,0:T(8,128)S(1)} %get-tuple-element.16.master, f32[2048,128]{1,0:T(8,128)S(1)} %get-tuple-element.17.moment, ...), custom_call_target="tpu_custom_call" | custom-call | tf_op jit(solution)/shard_map/results/pallas_call | solution.py:608

commit v6 on v5

--- a/solution.py
+++ b/solution.py
@@ -73,7 +73,7 @@
 WT = 32
 WAVE = 512
 ORDER = (
-    ("C", 2), ("S", 0, 2, 1), ("S", 0, 2, 0), ("C", 1), ("S", 1, 2, 1), ("S", 1, 1, 0), ("S", 0, 1, 1),
+     ("C", 1), ("S", 1, 2, 1), ("S", 1, 1, 0), ("S", 0, 1, 1),
     ("S", 1, 2, 0), ("S", 0, 1, 0), ("C", -1), ("S", 0, -1, 1), ("S", 0, -1, 0), ("C", 0), ("PX", 0, 2),
     ("S", 0, 0, 0), ("PX", 1, 1), ("PY", 0, 2), ("PY", 0, 3), ("PX", 1, 2), ("PX", 0, 1), ("PY", 1, 2),
     ("PY", 1, 3), ("PX", 0, -1), ("S", 1, -1, 0), ("FN", 0, 0, 0), ("PX", 0, 0), ("FN", 0, 0, 1),
@@ -131,7 +131,9 @@
     in_row = lax.broadcasted_iota(jnp.int32, (256, 256), 1)
     select = jnp.where(in_row == (out_row % 32) * 8 + out_row // 32, 1.0, 0.0).astype(BF)
     for p in range(4):
-        load_w[p].wait()
+        if p % 2 == 0:
+            load_w[p].wait()
+            load_w[p + 1].wait()
         if p == 2:
             for dy in (1, -1, 0):
                 load_f[0, dy].start()
@@ -197,9 +199,9 @@
         blocks = rv1.at[0, 0, 0, pl.ds(0, count)] if count <= 4 else rv1.at[0, pl.ds(0, count // 4), 0]
         remote(blocks, blocks, sent.at[0], sem, {X: ring(x, 1)}).wait_recv()
 
-    def chunk(dy):
-        rows = []
-        for w in range(2):
+    def chunk(dy, waves=(0, 1), ready=None):
+        rows, n = [], 128 * len(waves)
+        for w in waves:
             load_f[w, dy].wait()
             rows.append(pl.ds(mul_of(ring(y, dy) * 128 + WAVE * w, 128), 128))
         f = jnp.concatenate([feat[r, :] for r in rows], axis=0)
@@ -207,14 +209,16 @@
             gu = jnp.dot(f, w4[c], preferred_element_type=F32)
             gate, up = gu[:, :128], gu[:, 128:]
             value = (gate * jax.nn.sigmoid(gate) * up).astype(BF)
-            hid[:, c * 128:(c + 1) * 128] = value
-            for w in range(2):
-                both[c, rows[w], :] = gu[128 * w:128 * (w + 1)]
-        v = hid[...]
-        for h in range(4):
+            hid[0:n, c * 128:(c + 1) * 128] = value
+            for i, r in enumerate(rows):
+                both[c, r, :] = gu[128 * i:128 * (i + 1)]
+        v = hid[0:n, :]
+        for h in (2, 3, 0, 1):
             product = jnp.dot(v, down[:, h * 512:(h + 1) * 512], preferred_element_type=F32).astype(BF)
-            for w in range(2):
-                part[h, rows[w], :] = product[128 * w:128 * (w + 1)]
+            for i, r in enumerate(rows):
+                part[h, r, :] = product[128 * i:128 * (i + 1)]
+            if ready is not None and h % 2 == 1:
+                ready(h)
 
     def send(w, dy, q):
         if q == 0:
@@ -340,6 +344,14 @@
     steps = {"C": chunk, "S": send, "PX": pass_x, "PY": pass_y, "FN": finish, "L": loss_of, "G0": gather_0,
              "G0b": lambda w, q: spread(w, 0, q), "G1": gather_1, "G2": gather_2, "G3": gather_3, "R": relay, "B": backward,
              "T": first_columns}
+
+    def first_sends(h):
+        if h == 3:
+            greeted(dp_peers + mp_peers)
+        send(0, 2, h // 2)
+
+    chunk(2, (0,), first_sends)
+    chunk(2, (1,))
     for at, (name, *args) in enumerate(ORDER):
         if name == "FN" and not own:
             for c in small:
@@ -347,7 +359,6 @@
             own.extend(own_targets(2 * w + y // 2, (y % 2) * 128 + x * WT, rew, old, dones, lengths) for w in range(2))
         steps[name](*args)
         if at == 0:
-            greeted(dp_peers + mp_peers)
             small.extend(load(a, b) for a, b in ((head_hbm, head), (rew_hbm, rew), (old_hbm, old), (dones_hbm, dones),
                                                  (lengths_hbm, lengths)))
             state.extend(load(a, b) for a, b in ((master_hbm, master), (moment_hbm, moment), (second_hbm, second)))

time: 118 us -> 118 us (level)
  no operation moved by 1% of the time
where the time goes in v6:
time: 118 us
  Pallas kernels  117 us (99%)
    pallas_call x1, Pallas kernels, per_device(): pl.pallas_call(step_kernel, name='critic_step', out_shape=(pltpu.VMEM((8...  114 us
    pallas_call x1, Pallas kernels, per_device(): pl.pallas_call(tail_kernel, name='results', out_shape=(jax.ShapeDtypeStru...  3.59 us

profile of v6, /device:TPU:1, one launch (start us, length us, event | category | flops | bytes accessed | tf_op | source)
XLA Modules:
  0.0 118.2 jit_solution(1291747902387866425)
XLA Ops:
  0.6 113.8 %critic_step.1 = (bf16[16384,128]{1,0:T(8,128)(2,1)S(1)}, f32[2048,128]{1,0:T(8,128)S(1)}, f32[2048,128]{1,0:T(8,128)S(1)}, f32[2048,128]{1,0:T(8,128)S(1)}, f32[8,128]{1,0:T(8,128)S(1)}) custom-call(bf16[1024,2048]{1,0:T(8,128)(2,1)} %feat_hbm.1, bf16[16384,128]{1,0:T(8,128)(2,1)} %bitcast.42, bf16[512,2048]{1,0:T(8,128)(2,1)} %down_hbm.1, ...), custom_call_target="tpu_custom_call" | custom-call | tf_op jit(solution)/shard_map/critic_step/pallas_call | solution.py:595
  114.4 3.6 %results.1 = (bf16[16384,128]{1,0:T(8,128)(2,1)}, f32[2048,128]{1,0:T(8,128)}, f32[2048,128]{1,0:T(8,128)}, f32[2048,128]{1,0:T(8,128)}, f32[1,1]{1,0:T(1,128)}) custom-call(bf16[16384,128]{1,0:T(8,128)(2,1)S(1)} %get-tuple-element.15.work, f32[2048,128]{1,0:T(8,128)S(1)} %get-tuple-element.16.master, f32[2048,128]{1,0:T(8,128)S(1)} %get-tuple-element.17.moment, ...), custom_call_target="tpu_custom_call" | custom-call | tf_op jit(solution)/shard_map/results/pallas_call | solution.py:619

commit v7 on v6

--- a/solution.py
+++ b/solution.py
@@ -131,9 +131,7 @@
     in_row = lax.broadcasted_iota(jnp.int32, (256, 256), 1)
     select = jnp.where(in_row == (out_row % 32) * 8 + out_row // 32, 1.0, 0.0).astype(BF)
     for p in range(4):
-        if p % 2 == 0:
-            load_w[p].wait()
-            load_w[p + 1].wait()
+        load_w[p].wait()
         if p == 2:
             for dy in (1, -1, 0):
                 load_f[0, dy].start()

time: 118 us -> 118 us (level)
  no operation moved by 1% of the time
where the time goes in v7:
time: 118 us
  Pallas kernels  117 us (99%)
    pallas_call x1, Pallas kernels, per_device(): pl.pallas_call(step_kernel, name='critic_step', out_shape=(pltpu.VMEM((8...  114 us
    pallas_call x1, Pallas kernels, per_device(): pl.pallas_call(tail_kernel, name='results', out_shape=(jax.ShapeDtypeStru...  3.59 us

profile of v7, /device:TPU:1, one launch (start us, length us, event | category | flops | bytes accessed | tf_op | source)
XLA Modules:
  0.0 118.2 jit_solution(6855462610035030451)
XLA Ops:
  0.6 113.8 %critic_step.1 = (bf16[16384,128]{1,0:T(8,128)(2,1)S(1)}, f32[2048,128]{1,0:T(8,128)S(1)}, f32[2048,128]{1,0:T(8,128)S(1)}, f32[2048,128]{1,0:T(8,128)S(1)}, f32[8,128]{1,0:T(8,128)S(1)}) custom-call(bf16[1024,2048]{1,0:T(8,128)(2,1)} %feat_hbm.1, bf16[16384,128]{1,0:T(8,128)(2,1)} %bitcast.42, bf16[512,2048]{1,0:T(8,128)(2,1)} %down_hbm.1, ...), custom_call_target="tpu_custom_call" | custom-call | tf_op jit(solution)/shard_map/critic_step/pallas_call | solution.py:593
  114.4 3.6 %results.1 = (bf16[16384,128]{1,0:T(8,128)(2,1)}, f32[2048,128]{1,0:T(8,128)}, f32[2048,128]{1,0:T(8,128)}, f32[2048,128]{1,0:T(8,128)}, f32[1,1]{1,0:T(1,128)}) custom-call(bf16[16384,128]{1,0:T(8,128)(2,1)S(1)} %get-tuple-element.15.work, f32[2048,128]{1,0:T(8,128)S(1)} %get-tuple-element.16.master, f32[2048,128]{1,0:T(8,128)S(1)} %get-tuple-element.17.moment, ...), custom_call_target="tpu_custom_call" | custom-call | tf_op jit(solution)/shard_map/results/pallas_call | solution.py:617
